TPU v7x, 128 devices: a whole 4x4x4 slice. The times are simulated.
128 devices in a mesh: node: 4 (over z), chip: 32 (over x, y, core).
Axes of the slice: x: 4, y: 4, z: 4, core: 2. Of those that a mesh axis runs over, the one named last changes fastest.
Arguments:
- pooled_grad: bfloat16 [8192, 4, 256], P(('node', 'chip')), may hold values from -6 to 6
- grad_scale: bfloat16 [8192, 4], P(('node', 'chip')), may hold values from 0.049804688 to 1
- hot_slot: int32 [8192, 4, 2], P(('node', 'chip')), may hold values from 0 to 511
- send_index: int32 [128, 128, 32], P(('node', 'chip')), may hold values from 0 to 255, as said below
- recv_row: int32 [128, 128, 32], P(('node', 'chip')), may hold values from 0 to 4096, as said below
- cold_weight: float32 [4, 131072, 256], P(None, ('node', 'chip')), may hold values from -3 to 3
- cold_accum: float32 [4, 131072], P(None, ('node', 'chip')), may hold values from 0.5 to 8
- hot_weight: float32 [4, 512, 256], replicated, may hold values from -3 to 3
- hot_accum: float32 [4, 512], replicated, may hold values from 1 to 64
Outputs:
- cold_weight_new: float32 [4, 131072, 256], P(None, ('node', 'chip'))
- cold_accum_new: float32 [4, 131072], P(None, ('node', 'chip'))
- hot_weight_new: float32 [4, 512, 256], replicated
- hot_accum_new: float32 [4, 512], replicated
Inputs may be any that keep to these rules, and one draw needn't show every extreme that they name: send_index and recv_row describe the same lookups: slot c from p to q is filled exactly when recv_row[q, p, c] < 4096, the filled slots of a pair come first, and the table in both entries agrees; some owners receive all 32 slots filled from every sender in every draw. `recv_row`: see send_index; empty slots hold 4096.
All inputs are finite; a program needn't handle non-finite values.
Results may differ from a plain program's by a relative error of at most 0.0003.
Values may be sent and summed in bfloat16 or wider, within the bound.
A program may use at most 64 MiB of HBM per device.

v0:
```python
import math

import jax
import jax.numpy as jnp
from jax import lax
from jax.sharding import Mesh
from jax.sharding import PartitionSpec as P

NODE_CHIP = ("node", "chip_0", "chip_1", "chip_2")


LEARN_RATE = 0.5


def in_one_piece(arrays, axis, split_dim, concat_dim, along):
    widths = [math.prod(a.shape[along:]) for a in arrays]
    both = jnp.concatenate(
        [a.reshape(*a.shape[:along], w) for a, w in zip(arrays, widths)], axis=along
    )
    result = lax.all_to_all(both, axis, split_axis=split_dim, concat_axis=concat_dim, tiled=True)
    pieces = jnp.split(result, [sum(widths[:k]) for k in range(1, len(widths))], axis=along)
    return tuple(
        (b.reshape(*result.shape[:along], *a.shape[along:]) for a, b in zip(arrays, pieces))
    )


def split_up(array, dim, peers):
    shape = array.shape
    pieces = array.reshape(*shape[:dim], peers, shape[dim] // peers, *shape[dim + 1 :])
    return jnp.moveaxis(pieces, dim, 0)


def sum_at_owner(array, axis, dim):
    peers = lax.axis_size(axis)
    pieces = lax.all_to_all(split_up(array, dim, peers), axis, 0, 0, tiled=True)
    return jnp.sum(pieces, axis=0)


def summed_rows(array, axes, dim):
    far, near = axes
    pieces = split_up(array, dim, lax.axis_size(far))
    nearer = sum_at_owner(pieces, near, dim + 1)
    arrived = lax.all_to_all(nearer, far, split_axis=0, concat_axis=0, tiled=True)
    return arrived.sum(axis=0)


def padded_to(lines, peers):
    spare = -lines.shape[0] % peers
    if not spare:
        return lines
    return jnp.concatenate([lines, jnp.zeros((spare, *lines.shape[1:]), lines.dtype)])


def sent_to_all(array, axis):
    peers = lax.axis_size(axis)
    return lax.all_to_all(
        jnp.broadcast_to(array[None], (peers, *array.shape)), axis, 0, 0, tiled=True
    )


def in_order(pieces, dim):
    shape = list(pieces.shape[1:])
    shape[dim] *= pieces.shape[0]
    return jnp.moveaxis(pieces, 0, dim).reshape(shape)


def whole_of(array, axes, dim):
    far, near = axes
    leading = sent_to_all(array, far)
    pieces = jnp.swapaxes(sent_to_all(leading, near), 0, 1)
    return in_order(pieces.reshape(-1, *array.shape), dim)


def sum_by_parts(array, axes):
    lines = array.reshape(-1, array.shape[-1])
    own = summed_rows(padded_to(lines, lax.axis_size(axes[0]) * lax.axis_size(axes[1])), axes, 0)
    whole = whole_of(own, axes, 0)
    return whole[: len(lines)].reshape(array.shape)


def adagrad(weight, accum, grad):
    accum_new = accum + jnp.mean(grad * grad, axis=-1)
    return (weight - LEARN_RATE * grad / jnp.sqrt(accum_new)[..., None], accum_new)


def per_device(
    pooled_grad,
    grad_scale,
    hot_slot,
    send_index,
    recv_row,
    cold_weight,
    cold_accum,
    hot_weight,
    hot_accum,
):
    b_dev, tables, width = pooled_grad.shape
    devices = send_index.shape[1]
    capacity = send_index.shape[2]
    source_rows = b_dev * tables
    pooled_rows = pooled_grad.reshape(source_rows, width)
    scale_rows = grad_scale.reshape(source_rows, 1)
    chosen = send_index.reshape(devices * capacity)
    selector = (chosen[:, None] == jnp.arange(source_rows, dtype=jnp.int32)[None, :]).astype(
        jnp.bfloat16
    )
    outgoing = jnp.dot(selector, pooled_rows, preferred_element_type=jnp.float32).astype(
        jnp.bfloat16
    )
    out_scale = (
        jnp.dot(selector, scale_rows, preferred_element_type=jnp.float32)
        .astype(jnp.bfloat16)
        .reshape(devices * capacity)
    )
    arrived, arrived_scale = in_one_piece(
        (outgoing.reshape(devices, capacity, width), out_scale.reshape(devices, capacity)),
        NODE_CHIP,
        0,
        0,
        2,
    )
    slots = devices * capacity
    arrived_rows = arrived.reshape(slots, width)
    arrived_scale = arrived_scale.reshape(slots)
    targets = recv_row.reshape(slots)
    rows_dev = cold_weight.shape[1]
    local_rows = tables * rows_dev
    block = math.gcd(local_rows, 2048)
    blocks = local_rows // block

    def block_grad(first_row):
        levels = first_row + jnp.arange(block, dtype=jnp.int32)
        weights = jnp.where(
            levels[:, None] == targets[None, :], arrived_scale[None, :], jnp.zeros((), jnp.bfloat16)
        )
        return jnp.dot(weights, arrived_rows, preferred_element_type=jnp.float32)

    starts = jnp.arange(blocks, dtype=jnp.int32) * block
    cold_grad = lax.map(block_grad, starts).reshape(local_rows, width)
    new_weight, new_accum = adagrad(
        cold_weight.reshape(local_rows, width), cold_accum.reshape(local_rows), cold_grad
    )
    cold_weight_new = new_weight.reshape(tables, rows_dev, width)
    cold_accum_new = new_accum.reshape(tables, rows_dev)
    hot_rows = hot_weight.shape[1]
    levels = jnp.arange(hot_rows, dtype=jnp.int32)
    matches = jnp.sum((hot_slot[:, :, :, None] == levels).astype(jnp.float32), axis=2)
    coeffs = (matches * grad_scale.astype(jnp.float32)[:, :, None]).astype(jnp.bfloat16)
    hot_term = jnp.einsum("sth,std->thd", coeffs, pooled_grad, preferred_element_type=jnp.float32)
    hot_grad = sum_by_parts(hot_term, (("node", "chip_0", "chip_1"), "chip_2"))
    hot_weight_new, hot_accum_new = adagrad(hot_weight, hot_accum, hot_grad)
    return (cold_weight_new, cold_accum_new, hot_weight_new, hot_accum_new)


def solution(mesh):
    torus = Mesh(
        mesh.devices.reshape(mesh.shape["node"], 4, 4, 2), ("node", "chip_0", "chip_1", "chip_2")
    )
    in_specs = (
        P(NODE_CHIP, None, None),
        P(NODE_CHIP, None),
        P(NODE_CHIP, None, None),
        P(NODE_CHIP, None, None),
        P(NODE_CHIP, None, None),
        P(None, NODE_CHIP, None),
        P(None, NODE_CHIP),
        P(),
        P(),
    )
    out_specs = (P(None, NODE_CHIP, None), P(None, NODE_CHIP), P(), P())
    return jax.shard_map(
        per_device, mesh=torus, in_specs=in_specs, out_specs=out_specs, check_vma=False
    )
```

profile of v0, /device:TPU:1, one launch (start us, length us, event | category | flops | bytes accessed | tf_op | source)
XLA Modules:
  0.0 147.0 jit_solution(5754051126708176079)
XLA Ops:
  0.6 0.9 convert_reduce_fusion
  2.2 1.5 %fusion.11 = f32[4,512,256]{2,1,0:T(8,128)S(1)} fusion(f32[64,4,512]{2,0,1:T(8,128)S(1)} %convert_reduce_fusion, f32[64,4]{0,1:T(4,128)S(1)} %convert_element_type.20, bf16[64,4,256]{2,1,0:T(4,128)(2,1)} %param.11), kind=kOutput, calls=%fused_computation.26 | convolution fusion | flops 67371008 | bytes 2753536 | tf_op jit(solution)/shard_map/sth,std->thd/dot_general | solution.py:149
  3.9 6.4 %all_to_all.25 = f32[2,64,16,256]{3,2,1,0:T(8,128)S(1)} all-to-all(f32[2,64,16,256]{3,2,1,0:T(8,128)S(1)} %bitcast.35), channel_id=1, replica_groups=mesh['node'=4,'chip_0'=4,'chip_1'=4,'chip_2'=2] {'chip_2'}, dimensions={0} | all-to-all | bytes 4194304 | tf_op jit(solution)/shard_map/all_to_all | solution.py:35
  10.6 28.7 %all_to_all.26 = f32[64,16,256]{2,1,0:T(8,128)S(1)} all-to-all(f32[64,16,256]{2,1,0:T(8,128)S(1)} %reduce_sum.47), channel_id=1, replica_groups=mesh['node'=4,'chip_0'=4,'chip_1'=4,'chip_2'=2] {'node','chip_0','chip_1'}, dimensions={0} | all-to-all | bytes 2097152 | tf_op jit(solution)/shard_map/all_to_all | solution.py:43
  39.5 1.1 broadcast_in_dim.26
  40.6 4.7 %all-to-all-start.3 = ((f32[64,16,256]{2,1,0:T(8,128)}), f32[64,16,256]{2,1,0:T(8,128)S(1)}, u32[]{:S(2)}, u32[]{:S(2)}) async-start(f32[64,16,256]{2,1,0:T(8,128)} %broadcast_in_dim.26), calls=%async_computation.3 | async-start | bytes 2097152 | tf_op jit(solution)/shard_map/all_to_all | solution.py:56
  45.7 1.0 fusion.8
  46.8 2.1 %reshape_reshape_reshape.9 = bf16[128,32,1]{2,1,0:T(8,128)(2,1)S(1)} reshape(bf16[4096]{0:T(1024)(128)(2,1)S(1)} %convert_element_type.18) | data formatting | bytes 16384 | tf_op jit(solution)/shard_map/reshape;reshape;reshape | solution.py:18
  48.9 2.2 %convolution_convert_fusion = bf16[4096,256]{1,0:T(8,128)(2,1)S(1)} fusion(bf16[256,256]{1,0:T(8,128)(2,1)S(1)} %reshape.71, s32[4096]{0:T(1024)S(1)} %eq.43), kind=kOutput, calls=%fused_computation.10 | convolution fusion | flops 538968064 | bytes 2244608 | tf_op jit(solution)/shard_map/dot_general | solution.py:107
  51.1 2.2 %pad_maximum_fusion = bf16[128,32,257]{2,1,0:T(8,128)(2,1)} fusion(bf16[128,32,1]{2,1,0:T(8,128)(2,1)S(1)} %reshape_reshape_reshape.9, bf16[128,32,256]{2,1,0:T(8,128)(2,1)S(1)} %bitcast.36), kind=kLoop, calls=%fused_computation.15 | loop fusion | flops 4210688 | bytes 4210688 | tf_op jit(solution)/shard_map/concatenate | solution.py:17
  53.4 8.0 %all-to-all-done.3 = f32[64,16,256]{2,1,0:T(8,128)S(1)} async-done(((f32[64,16,256]{2,1,0:T(8,128)}), f32[64,16,256]{2,1,0:T(8,128)S(1)}, u32[]{:S(2)}, u32[]{:S(2)}) %all-to-all-start.3) | async-done | bytes 1048608 | tf_op jit(solution)/shard_map/all_to_all | solution.py:56
  61.6 8.7 %all_to_all.27 = f32[2,64,16,256]{3,2,1,0:T(8,128)S(1)} all-to-all(f32[2,64,16,256]{3,2,1,0:T(8,128)S(1)} %broadcast_in_dim.42), channel_id=1, replica_groups=mesh['node'=4,'chip_0'=4,'chip_1'=4,'chip_2'=2] {'chip_2'}, dimensions={0} | all-to-all | bytes 4194304 | tf_op jit(solution)/shard_map/all_to_all | solution.py:56
  70.3 5.0 %all-to-all-start = ((bf16[128,32,257]{2,1,0:T(8,128)(2,1)}), bf16[128,32,257]{2,1,0:T(8,128)(2,1)}, u32[]{:S(2)}, u32[]{:S(2)}) async-start(bf16[128,32,257]{2,1,0:T(8,128)(2,1)} %pad_maximum_fusion), calls=%async_computation | async-start | bytes 6291456 | tf_op jit(solution)/shard_map/all_to_all | solution.py:20
  76.9 0.8 copy-done
  77.7 1.7 %divide_subtract_fusion.1 = f32[4,512,256]{2,1,0:T(8,128)} fusion(f32[4,512,256]{2,1,0:T(8,128)S(1)} %copy-done, f32[4,512,256]{2,1,0:T(8,128)S(1)} %bitcast.34, f32[4,512]{1,0:T(4,128)S(1)} %get-tuple-element.79), kind=kLoop, calls=%fused_computation.18 | loop fusion | flops 1048576 | bytes 6299648 | tf_op jit(solution)/shard_map/sub | solution.py:83
  79.3 37.4 %all-to-all-done = bf16[128,32,257]{2,1,0:T(8,128)(2,1)} async-done(((bf16[128,32,257]{2,1,0:T(8,128)(2,1)}), bf16[128,32,257]{2,1,0:T(8,128)(2,1)}, u32[]{:S(2)}, u32[]{:S(2)}) %all-to-all-start) | async-done | bytes 2105376 | tf_op jit(solution)/shard_map/all_to_all | solution.py:20
  116.8 1.3 split.8
  118.1 0.8 copy.61
  119.0 1.8 %split.9 = bf16[128,32,256]{2,1,0:T(8,128)(2,1)S(1)} slice(bf16[128,32,257]{2,1,0:T(8,128)(2,1)} %all-to-all-done), slice={[0:128], [0:32], [0:256]} | slice | bytes 4194304 | tf_op jit(solution)/shard_map/split | solution.py:21
  120.8 15.7 %while.11 = (s32[]{:T(128)}, f32[2,2048,256]{2,1,0:T(8,128)}, s32[2]{0:T(128)S(1)}, s32[1,128,32]{2,1,0:T(8,128)}, bf16[128,32,1]{1,0,2:T(8,128)(2,1)}, /*index=...) while((s32[]{:T(128)}, f32[2,2048,256]{2,1,0:T(8,128)}, ...), condition=%wide.wide.region_1.2_spmd, body=%wide.wide.region_0.1_spmd.sunk | while | flops 4311746560 | bytes 4235885 | solution.py:139
  122.1 6.5 %fusion.24 = f32[2,2048,256]{2,1,0:T(8,128)} fusion(f32[2,2048,256]{2,1,0:T(8,128)} %get-tuple-element.167, s32[]{:T(128)} %get-tuple-element.166, bf16[4096,256]{1,0:T(8,128)(2,1)S(1)} %get-tuple-element.180, s32[4096]{0:T(1024)S(1)} %get-tuple-element.181, s32[2048]{0:T(1024)S(1)} %iota_add_fusion.3, bf16[4096]{0:T(1024)(128)(2,1)S(1)} %get-tuple-element.182), kind=kOutput, calls=%fused_computation.7.clone.clone.1 | convolution fusion | flops 4311744512 | bytes 4227584 | tf_op jit(solution)/shard_map/while/body/eval_jaxpr/dot_general | solution.py:136
  130.0 6.5 %fusion.24 = f32[2,2048,256]{2,1,0:T(8,128)} fusion(f32[2,2048,256]{2,1,0:T(8,128)} %get-tuple-element.167, s32[]{:T(128)} %get-tuple-element.166, bf16[4096,256]{1,0:T(8,128)(2,1)S(1)} %get-tuple-element.180, s32[4096]{0:T(1024)S(1)} %get-tuple-element.181, s32[2048]{0:T(1024)S(1)} %iota_add_fusion.3, bf16[4096]{0:T(1024)(128)(2,1)S(1)} %get-tuple-element.182), kind=kOutput, calls=%fused_computation.7.clone.clone.1 | convolution fusion | flops 4311744512 | bytes 4227584 | tf_op jit(solution)/shard_map/while/body/eval_jaxpr/dot_general | solution.py:136
  136.5 4.7 %multiply_reduce_fusion = (f32[2,2048]{1,0:T(2,128)S(1)}, f32[2,2048,256]{2,1,0:T(8,128)}) fusion(f32[2,2048,256]{2,1,0:T(8,128)} %get-tuple-element.36), kind=kLoop, calls=%fused_computation.12 | loop fusion | flops 3141632 | bytes 8404992 | tf_op jit(solution)/shard_map/reduce_sum | solution.py:82
  141.8 5.1 %divide_subtract_fusion = f32[4,1024,256]{2,1,0:T(8,128)} fusion(f32[4,1024,256]{2,1,0:T(8,128)} %param.16, f32[4,1024,256]{2,1,0:T(8,128)} %bitcast.32, f32[4,1024]{1,0:T(4,128)S(1)} %get-tuple-element.81), kind=kLoop, calls=%fused_computation.11 | loop fusion | flops 2097152 | bytes 12599296 | tf_op jit(solution)/shard_map/sub | solution.py:83
  (46 shorter events, 6.9 us)
Async XLA Ops:
  10.4 34.9 %copy-start.1 = (bf16[64,4,256]{2,1,0:T(4,128)(2,1)S(1)}, bf16[64,4,256]{2,1,0:T(4,128)(2,1)}, u32[]{:S(2)}) copy-start(bf16[64,4,256]{2,1,0:T(4,128)(2,1)} %param.11) | copy-start | bytes 393220
  10.4 35.0 %copy-start.8 = (bf16[64,4]{0,1:T(4,128)(2,1)S(1)}, bf16[64,4]{0,1:T(4,128)(2,1)}, u32[]{:S(2)}) copy-start(bf16[64,4]{0,1:T(4,128)(2,1)} %param.12) | copy-start | bytes 1540
  10.4 35.1 %copy-start.4 = (s32[1,128,32]{1,2,0:T(8,128)S(1)}, s32[1,128,32]{1,2,0:T(8,128)}, u32[]{:S(2)}) copy-start(s32[1,128,32]{1,2,0:T(8,128)} %param.14) | copy-start | bytes 49156
  40.6 20.8 %all-to-all-start.3 = ((f32[64,16,256]{2,1,0:T(8,128)}), f32[64,16,256]{2,1,0:T(8,128)S(1)}, u32[]{:S(2)}, u32[]{:S(2)}) async-start(f32[64,16,256]{2,1,0:T(8,128)} %broadcast_in_dim.26), calls=%async_computation.3 | async-start | bytes 2097152 | tf_op jit(solution)/shard_map/all_to_all | solution.py:56
  70.3 5.0 %copy-start.5 = (s32[1,128,32]{1,2,0:T(8,128)S(1)}, s32[1,128,32]{1,2,0:T(8,128)}, u32[]{:S(2)}) copy-start(s32[1,128,32]{1,2,0:T(8,128)} %param.15) | copy-start | bytes 49156
  70.3 5.8 %copy-start.7 = (f32[4,512]{1,0:T(4,128)S(1)}, f32[4,512]{1,0:T(4,128)}, u32[]{:S(2)}) copy-start(f32[4,512]{1,0:T(4,128)} %param.19) | copy-start | bytes 24580
  70.3 46.5 %all-to-all-start = ((bf16[128,32,257]{2,1,0:T(8,128)(2,1)}), bf16[128,32,257]{2,1,0:T(8,128)(2,1)}, u32[]{:S(2)}, u32[]{:S(2)}) async-start(bf16[128,32,257]{2,1,0:T(8,128)(2,1)} %pad_maximum_fusion), calls=%async_computation | async-start | bytes 6291456 | tf_op jit(solution)/shard_map/all_to_all | solution.py:20
  75.4 3.9 %copy-start.2 = (s32[1,128,32]{2,1,0:T(8,128)}, s32[1,128,32]{2,1,0:T(8,128)S(1)}, u32[]{:S(2)}) copy-start(s32[1,128,32]{2,1,0:T(8,128)S(1)} %copy.60) | copy-start | bytes 49156
  76.1 1.6 %copy-start = (f32[4,512,256]{2,1,0:T(8,128)S(1)}, f32[4,512,256]{2,1,0:T(8,128)}, u32[]{:S(2)}) copy-start(f32[4,512,256]{2,1,0:T(8,128)} %param.18) | copy-start | bytes 6291460
  118.9 1.9 %copy-start.3 = (bf16[128,32,1]{1,0,2:T(8,128)(2,1)}, bf16[128,32,1]{1,0,2:T(8,128)(2,1)S(1)}, u32[]{:S(2)}) copy-start(bf16[128,32,1]{1,0,2:T(8,128)(2,1)S(1)} %copy.61) | copy-start | bytes 24580
  136.5 4.8 %copy-start.6 = (f32[4,1024]{1,0:T(4,128)S(1)}, f32[4,1024]{1,0:T(4,128)}, u32[]{:S(2)}) copy-start(f32[4,1024]{1,0:T(4,128)} %param.17) | copy-start | bytes 49156
where the time goes:
time: 148 us; the launch traced here: 147 us
  waiting for transfers between devices  45.4 us (31%)
  blocking collectives  43.8 us (30%)
  other arithmetic  18.9 us (13%)
  matrix products  17.8 us (12%)
  local copies, waits for them, and re-layouts  10.6 us (7%)
  starting transfers between devices  9.7 us (7%)
    all_to_all x1, waiting for transfers between devices, in_one_piece(): lax.all_to_all(both, axis, split_axis=split_dim, concat_axis=concat_dim,...  37.4 us
    all_to_all x1, blocking collectives, summed_rows(): lax.all_to_all(nearer, far, split_axis=0, concat_axis=0, tiled=True)  28.7 us
    dot_general x2, matrix products, block_grad(): return jnp.dot(weights, arrived_rows, preferred_element_type=jnp.float32)  13 us
    all_to_all x1, blocking collectives, sent_to_all(): lax.all_to_all(jnp.broadcast_to(array[None], (peers, *array.shape)), axis...  8.65 us
    all_to_all x1, waiting for transfers between devices, sent_to_all(): lax.all_to_all(jnp.broadcast_to(array[None], (peers, *array.shape)), axis...  7.97 us
    sub x2, other arithmetic, adagrad(): weight - LEARN_RATE * grad / jnp.sqrt(accum_new)[..., None]  6.8 us
    all_to_all x1, blocking collectives, sum_at_owner(): pieces = lax.all_to_all(split_up(array, dim, peers), axis, 0, 0, tiled=True)  6.43 us
    reduce_sum x2, other arithmetic, adagrad(): accum_new = accum + jnp.mean(grad * grad, axis=-1)  5.06 us
  transfers between devices with their start and end apart: 2, of which 2 were waited for; matrix products, arithmetic and copies ran while one was open for 8% of the time, Pallas kernels for 0%

commit v1 on v0

v1 whole, which is shorter than its diff:
```python
import functools
import math

import jax
import jax.numpy as jnp
from jax import lax
from jax.experimental import pallas as pl
from jax.experimental.pallas import tpu as pltpu
from jax.sharding import PartitionSpec as P

NODE_CHIP = ("node", "chip")
MESH = pl.DeviceIdType.MESH
LEARN_RATE = 0.5
SEL = 256
META_ROWS = 48
BLOCK_ROWS = SEL + META_ROWS
ROW_STEP = 512
F32 = jnp.float32
BF16 = jnp.bfloat16


def row_of(tile, row):
    values = tile.astype(F32)
    at = lax.broadcasted_iota(jnp.int32, values.shape, 0) == row
    return jnp.sum(jnp.where(at, values, 0.0), axis=0, keepdims=True)


def exchange_kernel(
    rows, meta, targets, cold_grad, hot_grad,
    g, s, ssc, arrived, scr, hp, hr, hs,
    l0, s1, r1, s2, r2, s3, r3, s4, r4, s5, r5, s6, r6, s7, r7, s8, r8, s9, r9,
):
    z = lax.axis_index("node")
    k = lax.axis_index("chip")
    x, y, c = k // 8, (k // 2) % 4, k % 2
    p1 = y + c * (x - y)
    p2 = x + c * (y - x)
    mine = z * 2 + c
    column = x * 4 + y

    def plane(q1, q2):
        xx = q2 + c * (q1 - q2)
        yy = q1 + c * (q2 - q1)
        return (z, xx * 8 + yy * 2 + c)

    def share(q1, q2):
        xx = q2 + c * (q1 - q2)
        yy = q1 + c * (q2 - q1)
        return xx, yy

    def along_z(m):
        zz, cc = (z + m // 2) % 4, (c + m) % 2
        return zz * 2 + cc, (zz, x * 8 + y * 2 + cc)

    def from_z(m):
        zz, cc = (z + 4 - m // 2) % 4, (c + m) % 2
        return zz * 2 + cc, cc

    local = [
        pltpu.make_async_copy(rows, g.at[p2, p1, pl.ds(0, SEL)], l0.at[0]),
        pltpu.make_async_copy(meta, g.at[p2, p1, pl.ds(SEL, META_ROWS)], l0.at[1]),
    ]
    for copy in local:
        copy.start()

    barrier = pltpu.get_barrier_semaphore()
    for d in (1, 2, 3):
        pl.semaphore_signal(barrier, inc=1, device_id=plane((p1 + d) % 4, p2), device_id_type=MESH)
        pl.semaphore_signal(barrier, inc=1, device_id=plane(p1, (p2 + d) % 4), device_id_type=MESH)
    for m in range(1, 8):
        pl.semaphore_signal(barrier, inc=1, device_id=along_z(m)[1], device_id_type=MESH)
    pl.semaphore_wait(barrier, 13)
    for copy in local:
        copy.wait()

    sends = []

    def send(src, dst, ssem, rsem, dev):
        copy = pltpu.make_async_remote_copy(
            src, dst, ssem, rsem, device_id=dev, device_id_type=MESH
        )
        copy.start()
        sends.append(copy)

    def landed(dst, ssem, rsem):
        pltpu.make_async_remote_copy(
            dst, dst, ssem, rsem, device_id=plane(p1, p2), device_id_type=MESH
        ).wait_recv()

    own = g.at[p2, p1]
    for d in (1, 3, 2):
        send(own, own, s1.at[d], r1.at[d], plane((p1 + d) % 4, p2))
    for d in (1, 3, 2):
        send(own, own, s2.at[d, 0], r2.at[d, 0], plane(p1, (p2 + d) % 4))

    lanes = lax.broadcasted_iota(jnp.int32, (SEL, SEL), 1).astype(F32)
    groups = lax.broadcasted_iota(jnp.int32, (8, SEL), 0)
    owners = lax.broadcasted_iota(jnp.int32, (8, SEL), 1) // 32
    quarter = lax.broadcasted_iota(jnp.int32, (8, 128), 1) // 32
    levels = lax.broadcasted_iota(jnp.int32, (128, SEL), 0).astype(F32)

    def select(b, many):
        picks = [row_of(g[b, a, SEL : SEL + 16, :], column) for a in many]
        pad = [jnp.zeros((8 - len(many), SEL), F32)]
        turned = jnp.transpose(jnp.concatenate(picks + pad, axis=0))
        for n, a in enumerate(many):
            pick = jnp.where(turned[:, n : n + 1] == lanes, 1.0, 0.0).astype(BF16)
            got = jnp.dot(pick, g[b, a, 0:SEL, :], preferred_element_type=F32)
            s[:, b, a] = got.astype(BF16).reshape(8, 32, SEL)
            arrived[mine, b, a] = s[mine, b, a]

    def send_scales(b, chunk):
        total = jnp.zeros((8, 128), F32)
        for a in range(4):
            wide = jnp.where(
                groups == owners, row_of(g[b, a, SEL + 16 : SEL + 32, :], column), 0.0
            )
            half = wide[:, :128] + wide[:, 128:]
            half = half + pltpu.roll(half, 64, 1)
            half = half + pltpu.roll(half, 32, 1)
            total = total + jnp.where(quarter == a, half, 0.0)
        for q in range(8):
            ssc[b, q] = total[q : q + 1]
        scr[mine, b] = ssc[b, mine]
        for m in range(1, 8):
            to, dev = along_z(m)
            send(ssc.at[b, to], scr.at[mine, b], s4.at[m, chunk], r4.at[m, chunk], dev)

    def add_hot(b, first):
        total = jnp.zeros((128, SEL), F32)
        for a in range(4):
            info = g[b, a, SEL + 32 : SEL + 48, :].astype(F32)
            at0 = jnp.where(info[0:1] == column.astype(F32), info[1:2], -1.0)
            at1 = jnp.where(info[2:3] == column.astype(F32), info[3:4], -1.0)
            scale = info[4:5]
            weight = jnp.where(levels == at0, scale, 0.0) + jnp.where(levels == at1, scale, 0.0)
            total = total + jnp.dot(
                weight.astype(BF16), g[b, a, 0:SEL, :], preferred_element_type=F32
            )
        total = total.reshape(8, 16, SEL)
        hp[...] = total if first else hp[...] + total

    def scatter(offset, chunk, first):
        for m in range(1, 8):
            src, cc = from_z(m)
            b = (x + cc * (y - x) + 4 - offset) % 4
            if chunk == 0:
                for j in range(4):
                    a = (y + cc * (x - y) + 4 - j) % 4
                    landed(arrived.at[src, b, a], s3.at[m, j], r3.at[m, j])
            else:
                landed(arrived.at[src, b], s3.at[m, 3 + chunk], r3.at[m, 3 + chunk])
            landed(scr.at[src, b], s4.at[m, chunk], r4.at[m, chunk])
        wanted, scales, values = [], [], []
        for q in range(8):
            cc = q % 2
            b = (x + cc * (y - x) + 4 - offset) % 4
            wanted.append(targets[q, b])
            scales.append(scr[q, b])
            values.append(arrived[q, b].reshape(128, SEL))
        wanted = jnp.concatenate(wanted, axis=1)
        scales = jnp.concatenate(scales, axis=1)
        values = jnp.concatenate(values, axis=0)
        level = lax.broadcasted_iota(jnp.int32, (ROW_STEP, 1024), 0)

        def step(i, carry):
            at = pl.ds(pl.multiple_of(i * ROW_STEP, ROW_STEP), ROW_STEP)
            weight = jnp.where(level == wanted - i * ROW_STEP, scales, 0.0).astype(BF16)
            total = jnp.dot(weight, values, preferred_element_type=F32)
            cold_grad[at, :] = total if first else cold_grad[at, :] + total
            return carry

        lax.fori_loop(0, cold_grad.shape[0] // ROW_STEP, step, 0)

    def send_rows(b, a, slot):
        for m in range(1, 8):
            to, dev = along_z(m)
            if a is None:
                send(s.at[to, b], arrived.at[mine, b], s3.at[m, slot], r3.at[m, slot], dev)
            else:
                send(s.at[to, b, a], arrived.at[mine, b, a], s3.at[m, slot], r3.at[m, slot], dev)

    select(p2, [p1])
    send_rows(p2, p1, 0)
    for j in (1, 3, 2):
        a = (p1 + 4 - j) % 4
        landed(g.at[p2, a], s1.at[j], r1.at[j])
        for d in (1, 3, 2):
            send(g.at[p2, a], g.at[p2, a], s2.at[d, j], r2.at[d, j], plane(p1, (p2 + d) % 4))
        select(p2, [a])
        send_rows(p2, a, j)
    send_scales(p2, 0)
    add_hot(p2, True)

    def next_chunk(n, d):
        b = (p2 + 4 - d) % 4
        for j in (0, 1, 3, 2):
            landed(g.at[b, (p1 + 4 - j) % 4], s2.at[d, j], r2.at[d, j])
        if n == 3:
            add_hot(b, False)
            hr[mine] = hp[mine]
            for m in range(1, 8):
                to, dev = along_z(m)
                send(hp.at[to], hr.at[mine], s5.at[m], r5.at[m], dev)
        select(b, [0, 1, 2, 3])
        send_rows(b, None, 3 + n)
        send_scales(b, n)
        if n < 3:
            add_hot(b, False)

    next_chunk(1, 1)
    next_chunk(2, 3)
    scatter(0, 0, True)
    next_chunk(3, 2)
    scatter(1, 1, False)

    for m in range(1, 8):
        landed(hr.at[from_z(m)[0]], s5.at[m], r5.at[m])
    total = hr[0]
    for q in range(1, 8):
        total = total + hr[q]
    hs[...] = total
    hot_grad[x, y, mine] = total
    for m in range(1, 8):
        send(hs, hot_grad.at[x, y, mine], s6.at[m], r6.at[m], along_z(m)[1])
    scatter(3, 2, False)
    for m in range(1, 8):
        landed(hot_grad.at[x, y, from_z(m)[0]], s6.at[m], r6.at[m])

    part = pl.ds(c * 4, 4)
    twin_part = pl.ds(4 - c * 4, 4)
    twin = along_z(1)[1]
    piece = hot_grad.at[x, y, part]
    for d in (1, 3, 2):
        send(piece, piece, s7.at[d], r7.at[d], plane((p1 + d) % 4, p2))
    for d in (1, 3, 2):
        send(piece, piece, s8.at[d, 0], r8.at[d, 0], plane(p1, (p2 + d) % 4))
    for j in (1, 3, 2):
        xx, yy = share((p1 + 4 - j) % 4, p2)
        piece = hot_grad.at[xx, yy, part]
        landed(piece, s7.at[j], r7.at[j])
        for d in (1, 3, 2):
            send(piece, piece, s8.at[d, j], r8.at[d, j], plane(p1, (p2 + d) % 4))
        send(piece, piece, s9.at[0, j], r9.at[0, j], twin)
    scatter(2, 3, False)
    for d in (1, 3, 2):
        for j in (0, 1, 3, 2):
            xx, yy = share((p1 + 4 - j) % 4, (p2 + 4 - d) % 4)
            piece = hot_grad.at[xx, yy, part]
            landed(piece, s8.at[d, j], r8.at[d, j])
            send(piece, piece, s9.at[d, j], r9.at[d, j], twin)
    for d in range(4):
        for j in range(4):
            if d or j:
                q1 = (x + c * (y - x) + 4 - j) % 4
                q2 = (y + c * (x - y) + 4 - d) % 4
                xx = q1 + c * (q2 - q1)
                yy = q2 + c * (q1 - q2)
                landed(hot_grad.at[xx, yy, twin_part], s9.at[d, j], r9.at[d, j])
    for copy in sends:
        copy.wait_send()


def exchange(rows, meta, targets):
    dma = pltpu.SemaphoreType.DMA
    vmem = pl.BlockSpec(memory_space=pltpu.VMEM)
    hbm = pl.BlockSpec(memory_space=pl.ANY)
    return pl.pallas_call(
        exchange_kernel,
        out_shape=(
            jax.ShapeDtypeStruct((4096, 256), F32),
            jax.ShapeDtypeStruct((4, 4, 8, 16, 256), F32),
        ),
        in_specs=[hbm, hbm, vmem],
        out_specs=(vmem, vmem),
        scratch_shapes=[
            pltpu.VMEM((4, 4, BLOCK_ROWS, 256), BF16),
            pltpu.VMEM((8, 4, 4, 32, 256), BF16),
            pltpu.VMEM((4, 8, 1, 128), F32),
            pltpu.VMEM((8, 4, 4, 32, 256), BF16),
            pltpu.VMEM((8, 4, 1, 128), F32),
            pltpu.VMEM((8, 16, 256), F32),
            pltpu.VMEM((8, 16, 256), F32),
            pltpu.VMEM((16, 256), F32),
            dma((2,)),
            dma((4,)), dma((4,)),
            dma((4, 4)), dma((4, 4)),
            dma((8, 7)), dma((8, 7)),
            dma((8, 4)), dma((8, 4)),
            dma((8,)), dma((8,)),
            dma((8,)), dma((8,)),
            dma((4,)), dma((4,)),
            dma((4, 4)), dma((4, 4)),
            dma((4, 4)), dma((4, 4)),
        ],
        compiler_params=pltpu.CompilerParams(
            collective_id=0, has_side_effects=True, vmem_limit_bytes=48 * 1024 * 1024
        ),
        name="exchange",
    )(rows, meta, targets)


def adagrad_part(grad, weight, accum, weight_new, accum_new):
    eye = lax.broadcasted_iota(jnp.int32, (128, 128), 0) == lax.broadcasted_iota(
        jnp.int32, (128, 128), 1
    )
    for t in range(weight.shape[0]):
        for n in range(weight.shape[1] // 128):
            part = slice(n * 128, n * 128 + 128)
            value = grad[t, part, :]
            mean = jnp.sum(value * value, axis=1, keepdims=True) * (1.0 / value.shape[1])
            old = accum[t : t + 1, part]
            new = jnp.sum(jnp.where(eye, old, 0.0), axis=1, keepdims=True) + mean
            accum_new[t : t + 1, part] = jnp.sum(jnp.where(eye, new, 0.0), axis=0, keepdims=True)
            weight_new[t, part, :] = weight[t, part, :] - value * (LEARN_RATE / jnp.sqrt(new))


def update_kernel(
    cold_grad, cold_weight, cold_accum, hot_grad, hot_weight, hot_accum,
    cold_weight_new, cold_accum_new, hot_weight_new, hot_accum_new,
):
    adagrad_part(cold_grad, cold_weight, cold_accum, cold_weight_new, cold_accum_new)
    adagrad_part(hot_grad, hot_weight, hot_accum, hot_weight_new, hot_accum_new)


def update(cold_grad, cold_weight, cold_accum, hot_grad, hot_weight, hot_accum):
    steps = 4

    def blocks(array):
        shape = list(array.shape)
        shape[1] //= steps
        index = (lambda i: (0, i, 0)) if len(shape) == 3 else (lambda i: (0, i))
        return pl.BlockSpec(tuple(shape), index)

    outs = (cold_weight, cold_accum, hot_weight, hot_accum)
    args = (cold_grad, cold_weight, cold_accum, hot_grad, hot_weight, hot_accum)
    return pl.pallas_call(
        update_kernel,
        grid=(steps,),
        out_shape=tuple(jax.ShapeDtypeStruct(a.shape, F32) for a in outs),
        in_specs=[blocks(a) for a in args],
        out_specs=tuple(blocks(a) for a in outs),
        name="update",
    )(*args)


def meta_of(grad_scale, hot_slot, send_index):
    chosen = send_index.reshape(4, 4, 4, 2, 32).transpose(1, 2, 0, 3, 4).reshape(16, 256)
    sources = jnp.arange(256, dtype=jnp.int32)
    flat_scale = grad_scale.reshape(1, 256)
    out_scale = jnp.sum(
        jnp.where(chosen[:, :, None] == sources, flat_scale.astype(F32), 0.0), axis=-1
    )
    rows = hot_slot + (jnp.arange(4, dtype=jnp.int32) * 512)[None, :, None]
    rows = rows.transpose(2, 0, 1).reshape(2, 256)
    hot = jnp.stack([rows[0] // 128, rows[0] % 128, rows[1] // 128, rows[1] % 128])
    return jnp.concatenate(
        [
            chosen.astype(BF16),
            out_scale.astype(BF16),
            hot.astype(BF16),
            flat_scale,
            jnp.zeros((11, 256), BF16),
        ],
        axis=0,
    )


def per_device(
    pooled_grad,
    grad_scale,
    hot_slot,
    send_index,
    recv_row,
    cold_weight,
    cold_accum,
    hot_weight,
    hot_accum,
):
    width = cold_weight.shape[2]
    rows = pooled_grad.reshape(SEL, width)
    meta = meta_of(grad_scale, hot_slot, send_index)
    received = recv_row.reshape(4, 4, 4, 2, 32)
    targets = jnp.stack(
        [received[:, :, :, 0], received[:, :, :, 1].transpose(0, 2, 1, 3)], axis=1
    ).reshape(8, 4, 1, 128)
    cold_grad, hot_grad = exchange(rows, meta, targets)
    return update(
        cold_grad.reshape(cold_weight.shape),
        cold_weight,
        cold_accum,
        hot_grad.reshape(hot_weight.shape),
        hot_weight,
        hot_accum,
    )


def solution(mesh):
    in_specs = (
        P(NODE_CHIP, None, None),
        P(NODE_CHIP, None),
        P(NODE_CHIP, None, None),
        P(NODE_CHIP, None, None),
        P(NODE_CHIP, None, None),
        P(None, NODE_CHIP, None),
        P(None, NODE_CHIP),
        P(),
        P(),
    )
    out_specs = (P(None, NODE_CHIP, None), P(None, NODE_CHIP), P(), P())
    return jax.shard_map(
        per_device, mesh=mesh, in_specs=in_specs, out_specs=out_specs, check_vma=False
    )
```

time: 148 us -> 85.1 us (0.57)
  Pallas kernels: 0 us -> 75.3 us
  waiting for transfers between devices: 45.4 us -> 0 us
  blocking collectives: 43.8 us -> 0 us
  matrix products: 17.8 us -> 0 us
  other arithmetic: 18.9 us -> 2.12 us
  starting transfers between devices: 9.7 us -> 0 us
  local copies, waits for them, and re-layouts: 10.6 us -> 6.57 us
    pallas_call x0 -> x2, Pallas kernels: none -> 75.3 us  [the longest x1 67 us: exchange(): pl.pallas_call(exchange_kernel, out_shape=(jax.ShapeDtypeStruct((4096, 25...]
    all_to_all x2 -> x0, waiting for transfers between devices: 45.4 us -> none  [the longest x1 37.4 us: in_one_piece(): lax.all_to_all(both, axis, split_axis=split_dim, concat_axis=concat_dim,...]
    all_to_all x3 -> x0, blocking collectives: 43.8 us -> none  [the longest x1 28.7 us: summed_rows(): lax.all_to_all(nearer, far, split_axis=0, concat_axis=0, tiled=True)]
    dot_general x5 -> x0, matrix products: 17.8 us -> none  [the longest x2 13 us: block_grad(): return jnp.dot(weights, arrived_rows, preferred_element_type=jnp.float32)]
    all_to_all x2 -> x0, starting transfers between devices: 9.7 us -> none  [the longest x1 5 us: in_one_piece(): lax.all_to_all(both, axis, split_axis=split_dim, concat_axis=concat_dim,...]
    sub x2 -> x0, other arithmetic: 6.8 us -> none  [adagrad(): weight - LEARN_RATE * grad / jnp.sqrt(accum_new)[..., None]]
    reduce_sum x5 -> x1, other arithmetic: 6.31 us -> 1.29 us  [meta_of(): jnp.sum(jnp.where(chosen[:, :, None] == sources, flat_scale.astype(F32),...]
    split x2 -> x0, local copies, waits for them, and re-layouts: 3.06 us -> none  [in_one_piece(): jnp.split(result, [sum(widths[:k]) for k in range(1, len(widths))], axis=...]
  transfers between devices with their start and end apart: 2 -> 0, of which waited for: 2 -> 0; matrix products, arithmetic and copies ran while one was open for 8% -> 0% of each run, Pallas kernels for 0% -> 0%
where the time goes in v1:
time: 85.1 us; the launch traced here: 84.8 us
  Pallas kernels  75.3 us (88%)
  local copies, waits for them, and re-layouts  6.57 us (8%)
  other arithmetic  2.12 us (2%)
    pallas_call x1, Pallas kernels, exchange(): pl.pallas_call(exchange_kernel, out_shape=(jax.ShapeDtypeStruct((4096, 25...  67 us
    pallas_call x1, Pallas kernels, update(): pl.pallas_call(update_kernel, grid=(steps,), out_shape=tuple((jax.ShapeDt...  8.31 us
    unnamed x6, local copies, waits for them, and re-layouts  3.74 us

profile of v1, /device:TPU:1, one launch (start us, length us, event | category | flops | bytes accessed | tf_op | source)
XLA Modules:
  0.0 84.8 jit_solution(7910608291122327580)
XLA Ops:
  0.6 0.8 add_bitcast_fusion
  1.4 0.8 copy.33
  2.2 0.1 reshape.256
  2.3 0.1 copy.32
  2.4 0.1 squeeze.12
  2.5 0.1 copy.31
  2.6 0.1 squeeze.11
  2.8 0.8 copy.30
  3.6 0.1 reshape.261
  3.7 0.8 copy.28
  4.5 0.1 reshape.255
  4.6 1.3 %select_reduce_fusion = bf16[16,256]{1,0:T(8,128)(2,1)S(1)} fusion(f32[256]{0:T(256)S(1)} %reshape.261, s32[16,256]{1,0:T(8,128)S(1)} %reshape.255), kind=kLoop, calls=%fused_computation | loop fusion | flops 3141632 | bytes 25600 | tf_op jit(solution)/shard_map/reduce_sum | solution.py:351
  6.0 0.2 concatenate.4.meta
  6.1 0.8 copy.34
  6.9 0.1 fusion.4
  7.1 0.1 reshape.258.targets
  7.2 0.9 %reshape.253.rows = bf16[256,256]{1,0:T(8,128)(2,1)S(1)} reshape(bf16[64,4,256]{2,1,0:T(4,128)(2,1)} %param.9) | data formatting | bytes 262144 | tf_op jit(solution)/shard_map/reshape | solution.py:381
  8.1 67.0 %exchange.1 = (f32[4096,256]{1,0:T(8,128)}, f32[4,4,8,16,256]{4,3,2,1,0:T(8,128)S(1)}) custom-call(bf16[256,256]{1,0:T(8,128)(2,1)S(1)} %reshape.253.rows, bf16[48,256]{1,0:T(8,128)(2,1)S(1)} %concatenate.4.meta, s32[8,4,1,128]{3,2,1,0:T(1,128)S(1)} %reshape.258.targets), custom_call_target="tpu_custom_call" | custom-call | tf_op jit(solution)/shard_map/exchange/pallas_call | solution.py:268
  75.1 0.0 copy-start
  75.1 1.3 %copy-done = f32[4,4,8,16,256]{4,3,2,1,0:T(8,128)} copy-done((f32[4,4,8,16,256]{4,3,2,1,0:T(8,128)}, f32[4,4,8,16,256]{4,3,2,1,0:T(8,128)S(1)}, u32[]{:S(2)}) %copy-start) | copy-done | bytes 2097176
  76.4 8.3 %update.1 = (f32[4,1024,256]{2,1,0:T(8,128)}, f32[4,1024]{1,0:T(4,128)}, f32[4,512,256]{2,1,0:T(8,128)}, f32[4,512]{1,0:T(4,128)}) custom-call(f32[4,1024,256]{2,1,0:T(8,128)} %bitcast.17, f32[4,1024,256]{2,1,0:T(8,128)} %cold_weight.1, f32[4,1024]{1,0:T(4,128)} %cold_accum.1, f32[4,512,256]{2,1,0:T(8,128)} %bitcast.16, f32[4,512,256]{2,1,0:T(8,128)} %hot_weight.1, ...), custom_call_target="tpu_custom_call" | custom-call | tf_op jit(solution)/shard_map/update/pallas_call | solution.py:337
  (11 shorter events, 0.1 us)
Async XLA Ops:
  75.1 1.3 %copy-start = (f32[4,4,8,16,256]{4,3,2,1,0:T(8,128)}, f32[4,4,8,16,256]{4,3,2,1,0:T(8,128)S(1)}, u32[]{:S(2)}) copy-start(f32[4,4,8,16,256]{4,3,2,1,0:T(8,128)S(1)} %get-tuple-element.7) | copy-start | bytes 6291460

commit v2 on v0

v2 whole, which is shorter than its diff:
```python
import jax
import jax.numpy as jnp
from jax import lax
from jax.experimental import pallas as pl
from jax.experimental.pallas import tpu as pltpu
from jax.sharding import PartitionSpec as P

NODE_CHIP = ("node", "chip")
MESH = pl.DeviceIdType.MESH
LEARN_RATE = 0.5
SEL = 256
BLOCK_ROWS = 288
ROW_STEP = 512
F32 = jnp.float32
BF16 = jnp.bfloat16
FORWARD = (0, 3)
SECOND = (
    (1, 0), (3, 0), (1, 1), (3, 1), (2, 0), (1, 3), (3, 3), (2, 1), (1, 2), (3, 2), (2, 3), (2, 2),
)


def iota(shape, dim):
    return lax.broadcasted_iota(jnp.int32, shape, dim)


def row_of(tile, row):
    values = tile.astype(F32)
    return jnp.sum(jnp.where(iota(values.shape, 0) == row, values, 0.0), axis=0, keepdims=True)


def turned(tile):
    values = tile.astype(F32)
    return jnp.transpose(jnp.concatenate([values, jnp.zeros((96, 128), F32)], axis=0))


def adagrad_rows(value, weight, old):
    eye = iota((128, 128), 0) == iota((128, 128), 1)
    mean = jnp.sum(value * value, axis=1, keepdims=True) * (1.0 / value.shape[1])
    new = jnp.sum(jnp.where(eye, old, 0.0), axis=1, keepdims=True) + mean
    flat = jnp.sum(jnp.where(eye, new, 0.0), axis=0, keepdims=True)
    return weight - value * (LEARN_RATE / jnp.sqrt(new)), flat


def step_kernel(
    rows_in, send_in, scale_in, hot_in, recv_in, cold_weight, cold_accum_in, hot_weight, hot_accum_in,
    cold_new, cold_accum_new, hot_new, hot_accum_new,
    g, s, ssc, arrived, scr, hp, hr, hs, hz, hot_grad, st, tt, cold_w, hot_w,
    rows, send_t, scale_t, hot_t, recv_t, cold_accum, hot_accum, l0, s1, r1, s2, r2, s3, r3, s4, r4, s5, r5, s6, r6, s7, r7, s8, r8, s9, r9,
):
    z = lax.axis_index("node")
    k = lax.axis_index("chip")
    x, y, c = k // 8, (k // 2) % 4, k % 2
    p1 = y + c * (x - y)
    p2 = x + c * (y - x)
    mine = z * 2 + c
    column = x * 4 + y
    part = pl.ds(c * 4, 4)
    twin_part = pl.ds(4 - c * 4, 4)
    twin = (z, x * 8 + y * 2 + 1 - c)

    def plane(q1, q2):
        xx = q2 + c * (q1 - q2)
        yy = q1 + c * (q2 - q1)
        return (z, xx * 8 + yy * 2 + c)

    def share(q1, q2):
        xx = q2 + c * (q1 - q2)
        yy = q1 + c * (q2 - q1)
        return xx, yy

    def along_z(m):
        zz, cc = (z + m // 2) % 4, (c + m) % 2
        return zz * 2 + cc, (zz, x * 8 + y * 2 + cc)

    def from_z(m):
        zz, cc = (z + 4 - m // 2) % 4, (c + m) % 2
        return zz * 2 + cc, cc

    first = [
        pltpu.make_async_copy(src, dst, l0.at[n])
        for n, (src, dst) in enumerate(
            ((rows_in, rows), (send_in, send_t), (scale_in, scale_t), (hot_in, hot_t))
        )
    ]
    later = [
        pltpu.make_async_copy(src, dst, l0.at[4 + n])
        for n, (src, dst) in enumerate(
            (
                (recv_in, recv_t), (cold_accum_in, cold_accum), (hot_accum_in, hot_accum),
                (cold_weight, cold_w), (hot_weight, hot_w),
            )
        )
    ]
    for copy in first:
        copy.start()

    barrier = pltpu.get_barrier_semaphore()
    for d in (1, 2, 3):
        pl.semaphore_signal(barrier, inc=1, device_id=plane((p1 + d) % 4, p2), device_id_type=MESH)
        pl.semaphore_signal(barrier, inc=1, device_id=plane(p1, (p2 + d) % 4), device_id_type=MESH)
    for m in range(1, 8):
        pl.semaphore_signal(barrier, inc=1, device_id=along_z(m)[1], device_id_type=MESH)

    for copy in first:
        copy.wait()
    g[p2, p1, 0:SEL, :] = rows[...].astype(F32).reshape(SEL, SEL).astype(BF16)
    st[...] = turned(send_t[...])
    halves = []
    for half in range(2):
        total = jnp.zeros((16, 128), F32)
        for n in range(4):
            zc = half * 4 + n
            group = st[pl.ds((zc // 2) * 32 + zc % 2, 16, stride=2), :]
            total = total + (pltpu.roll(group, 32 * n, 1) if n else group)
        halves.append(total)
    g[p2, p1, SEL : SEL + 16, :] = jnp.concatenate(halves, axis=1).astype(BF16)
    pieces = []
    for t in range(4):
        slot0, slot1 = hot_t[t, 0:1, :], hot_t[t, 1:2, :]
        pieces.append(
            jnp.concatenate(
                [
                    (slot0 // 128 + t * 4).astype(F32),
                    (slot0 % 128).astype(F32),
                    (slot1 // 128 + t * 4).astype(F32),
                    (slot1 % 128).astype(F32),
                    scale_t[t : t + 1, :].astype(F32),
                    jnp.zeros((3, 64), F32),
                ],
                axis=0,
            )
        )
    info = jnp.concatenate(pieces, axis=1).astype(BF16)
    from_lane = iota((SEL, SEL), 0)
    order = jnp.where((from_lane % 64) * 4 + from_lane // 64 == iota((SEL, SEL), 1), 1.0, 0.0)
    info = jnp.dot(info, order.astype(BF16), preferred_element_type=F32)
    g[p2, p1, SEL + 16 : SEL + 32, :] = jnp.concatenate(
        [info, jnp.zeros((8, SEL), F32)], axis=0
    ).astype(BF16)
    pl.semaphore_wait(barrier, 13)

    sends = []

    def send(src, dst, ssem, rsem, dev):
        copy = pltpu.make_async_remote_copy(
            src, dst, ssem, rsem, device_id=dev, device_id_type=MESH
        )
        copy.start()
        sends.append(copy)

    def landed(dst, ssem, rsem):
        pltpu.make_async_remote_copy(
            dst, dst, ssem, rsem, device_id=plane(p1, p2), device_id_type=MESH
        ).wait_recv()

    own = g.at[p2, p1]
    for d in (1, 3, 2):
        send(own, own, s1.at[d], r1.at[d], plane((p1 + d) % 4, p2))
    for d in (1, 3):
        send(own, own, s2.at[d, 0], r2.at[d, 0], plane(p1, (p2 + d) % 4))
    for copy in later:
        copy.start()

    lanes = iota((SEL, SEL), 1).astype(F32)
    same_owner = iota((8, SEL), 0) == iota((8, SEL), 1) // 32
    quarter = iota((8, 128), 1) // 32
    levels = iota((128, SEL), 0).astype(F32)
    totals = [jnp.zeros((8, 128), F32)] * 4
    hp[...] = jnp.zeros_like(hp)

    def select(b, a, j):
        chosen = row_of(g[b, a, SEL : SEL + 16, :], column)
        chosen = jnp.transpose(jnp.concatenate([chosen, jnp.zeros((7, SEL), F32)], axis=0))
        pick = jnp.where(chosen[:, 0:1] == lanes, 1.0, 0.0).astype(BF16)
        got = jnp.dot(pick, g[b, a, 0:SEL, :], preferred_element_type=F32)
        s[:, b, a] = got.astype(BF16).reshape(8, 32, SEL)
        for m in range(1, 8):
            to, dev = along_z(m)
            slot = j[0] * 4 + j[1]
            send(s.at[to, b, a], arrived.at[mine, b, a], s3.at[m, slot], r3.at[m, slot], dev)
        arrived[mine, b, a] = s[mine, b, a]
        scale = jnp.broadcast_to(g[b, a, SEL + 16 : SEL + 32, :].astype(F32)[4:5], (16, SEL))
        wide = lax.dot_general(
            scale.astype(BF16), pick, (((1,), (1,)), ((), ())), preferred_element_type=F32
        )
        wide = jnp.where(same_owner, wide[0:8], 0.0)
        half = wide[:, :128] + wide[:, 128:]
        half = half + pltpu.roll(half, 64, 1)
        half = half + pltpu.roll(half, 32, 1)
        totals[j[1]] = totals[j[1]] + jnp.where(quarter == b, half, 0.0)

    def send_scales(j):
        a = (p1 + 4 - j) % 4
        for q in range(8):
            ssc[a, q] = totals[j][q : q + 1]
        for m in range(1, 8):
            to, dev = along_z(m)
            send(ssc.at[a, to], scr.at[mine, a], s4.at[m, j], r4.at[m, j], dev)
        scr[mine, a] = ssc[a, mine]

    def add_hot(b, a):
        info = g[b, a, SEL + 16 : SEL + 32, :].astype(F32)
        at0 = jnp.where(info[0:1] == column.astype(F32), info[1:2], -1.0)
        at1 = jnp.where(info[2:3] == column.astype(F32), info[3:4], -1.0)
        scale = info[4:5]
        weight = jnp.where(levels == at0, scale, 0.0) + jnp.where(levels == at1, scale, 0.0)
        total = jnp.dot(weight.astype(BF16), g[b, a, 0:SEL, :], preferred_element_type=F32)
        hp[...] += total.reshape(8, 16, SEL)

    def gathered(q, j):
        zz, cc = q // 2, q % 2
        a = (y + cc * (x - y) + 4 - j) % 4
        wanted = jnp.zeros((1, 128), F32)
        for b in range(4):
            row = tt[pl.ds(zz * 32 + (8 - 6 * cc) * b + (2 + 6 * cc) * a + cc, 1), :]
            wanted = wanted + (pltpu.roll(row, 32 * b, 1) if b else row)
        return wanted, scr[q, a], arrived[q, :, a].reshape(128, SEL)

    def scatter(j, first=False, last=False):
        for m in range(1, 8):
            src, cc = from_z(m)
            a = (y + cc * (x - y) + 4 - j) % 4
            for d in range(4):
                b = (x + cc * (y - x) + 4 - d) % 4
                slot = d * 4 + j
                landed(arrived.at[src, b, a], s3.at[m, slot], r3.at[m, slot])
            landed(scr.at[src, a], s4.at[m, j], r4.at[m, j])
        parts = [gathered(q, j) for q in range(8)]
        wanted = jnp.concatenate([p[0] for p in parts], axis=1)
        scales = jnp.concatenate([p[1] for p in parts], axis=1)
        values = jnp.concatenate([p[2] for p in parts], axis=0)
        level = iota((ROW_STEP, 1024), 0).astype(F32)

        def step(i, carry):
            t, low = i // 2, pl.multiple_of((i % 2) * ROW_STEP, ROW_STEP)
            base = (i * ROW_STEP).astype(F32)
            weight = jnp.where(level == wanted - base, scales, 0.0).astype(BF16)
            total = jnp.dot(weight, values, preferred_element_type=F32)
            if not first:
                total = cold_new[t, pl.ds(low, ROW_STEP), :] + total
            if not last:
                cold_new[t, pl.ds(low, ROW_STEP), :] = total
                return carry
            for n in range(ROW_STEP // 128):
                at = pl.ds(pl.multiple_of(low + n * 128, 128), 128)
                kept = cold_accum_new[:, at]
                fresh, flat = adagrad_rows(
                    total[n * 128 : n * 128 + 128], cold_w[t, at, :], row_of(cold_accum[:, at], t)
                )
                cold_new[t, at, :] = fresh
                cold_accum_new[:, at] = jnp.where(iota((4, 128), 0) == t, flat, kept)
            return carry

        lax.fori_loop(0, 4096 // ROW_STEP, step, 0)

    select(p2, p1, (0, 0))
    add_hot(p2, p1)
    for j in (1, 3, 2):
        a = (p1 + 4 - j) % 4
        landed(g.at[p2, a], s1.at[j], r1.at[j])
        for d in (1, 3):
            send(g.at[p2, a], g.at[p2, a], s2.at[d, j], r2.at[d, j], plane(p1, (p2 + d) % 4))
        select(p2, a, (0, j))
        add_hot(p2, a)

    for d, j in SECOND:
        b, a = (p2 + 4 - d) % 4, (p1 + 4 - j) % 4
        landed(g.at[b, a], s2.at[d, j], r2.at[d, j])
        onward = 1 if j in FORWARD else 3
        if d == onward:
            send(g.at[b, a], g.at[b, a], s2.at[2, j], r2.at[2, j], plane(p1, (p2 + d) % 4))
        add_hot(b, a)
        if (d, j) == SECOND[-1]:
            send(hp.at[twin_part], hr, s5.at[0], r5.at[0], twin)
        select(b, a, (d, j))
        if d == 2:
            send_scales(j)

    for copy in later:
        copy.wait()
    tt[...] = turned(recv_t[...])
    scatter(0, first=True)

    landed(hr, s5.at[0], r5.at[0])
    hs[...] = hp[part] + hr[...]
    for m in (2, 6, 4):
        send(hs, hz.at[m // 2], s6.at[m // 2], r6.at[m // 2], along_z(m)[1])

    scatter(1)

    for m in (1, 3, 2):
        landed(hz.at[m], s6.at[m], r6.at[m])
    hot_grad[x, y, part] = hs[...] + hz[1] + hz[2] + hz[3]
    piece = hot_grad.at[x, y, part]
    for d in (1, 3, 2):
        send(piece, piece, s7.at[d], r7.at[d], plane((p1 + d) % 4, p2))
    for d in (1, 3):
        send(piece, piece, s8.at[d, 0], r8.at[d, 0], plane(p1, (p2 + d) % 4))
    send(piece, piece, s9.at[0, 0], r9.at[0, 0], twin)

    scatter(3)

    for j in (1, 3, 2):
        xx, yy = share((p1 + 4 - j) % 4, p2)
        piece = hot_grad.at[xx, yy, part]
        landed(piece, s7.at[j], r7.at[j])
        for d in (1, 3):
            send(piece, piece, s8.at[d, j], r8.at[d, j], plane(p1, (p2 + d) % 4))
        send(piece, piece, s9.at[0, j], r9.at[0, j], twin)

    def second_piece(d, j):
        xx, yy = share((p1 + 4 - j) % 4, (p2 + 4 - d) % 4)
        piece = hot_grad.at[xx, yy, part]
        landed(piece, s8.at[d, j], r8.at[d, j])
        onward = 1 if j in FORWARD else 3
        if d == onward:
            send(piece, piece, s8.at[2, j], r8.at[2, j], plane(p1, (p2 + d) % 4))
        send(piece, piece, s9.at[d, j], r9.at[d, j], twin)

    second_piece(1, 0)
    second_piece(3, 0)
    scatter(2, last=True)
    for d, j in SECOND[2:]:
        second_piece(d, j)
    for d in range(4):
        for j in range(4):
            q1 = (x + c * (y - x) + 4 - j) % 4
            q2 = (y + c * (x - y) + 4 - d) % 4
            xx = q1 + c * (q2 - q1)
            yy = q2 + c * (q1 - q2)
            landed(hot_grad.at[xx, yy, twin_part], s9.at[d, j], r9.at[d, j])
    for t in range(4):
        for n in range(4):
            at = slice(n * 128, n * 128 + 128)
            fresh, flat = adagrad_rows(
                hot_grad[t, n].reshape(128, SEL), hot_w[t, at, :], hot_accum[t : t + 1, at]
            )
            hot_new[t, at, :] = fresh
            hot_accum_new[t : t + 1, at] = flat
    for copy in sends:
        copy.wait_send()


def step(*args):
    dma = pltpu.SemaphoreType.DMA
    vmem = pl.BlockSpec(memory_space=pltpu.VMEM)
    hbm = pl.BlockSpec(memory_space=pltpu.HBM)
    outs = args[5:]
    args = [pltpu.with_memory_space_constraint(a, pltpu.HBM) for a in args]
    return pl.pallas_call(
        step_kernel,
        out_shape=tuple(jax.ShapeDtypeStruct(a.shape, F32) for a in outs),
        in_specs=[hbm] * 9,
        out_specs=(vmem,) * 4,
        scratch_shapes=[
            pltpu.VMEM((4, 4, BLOCK_ROWS, SEL), BF16),
            pltpu.VMEM((8, 4, 4, 32, SEL), BF16),
            pltpu.VMEM((4, 8, 1, 128), F32),
            pltpu.VMEM((8, 4, 4, 32, SEL), BF16),
            pltpu.VMEM((8, 4, 1, 128), F32),
            pltpu.VMEM((8, 16, SEL), F32),
            pltpu.VMEM((4, 16, SEL), F32),
            pltpu.VMEM((4, 16, SEL), F32),
            pltpu.VMEM((4, 4, 16, SEL), F32),
            pltpu.VMEM((4, 4, 8, 16, SEL), F32),
            pltpu.VMEM((128, 128), F32),
            pltpu.VMEM((128, 128), F32),
            pltpu.VMEM(outs[0].shape, F32),
            pltpu.VMEM(outs[2].shape, F32),
            *(pltpu.VMEM(a.shape, a.dtype) for a in (*args[:5], args[6], args[8])),
            dma((9,)),
            dma((4,)), dma((4,)),
            dma((4, 4)), dma((4, 4)),
            dma((8, 16)), dma((8, 16)),
            dma((8, 4)), dma((8, 4)),
            dma((1,)), dma((1,)),
            dma((4,)), dma((4,)),
            dma((4,)), dma((4,)),
            dma((4, 4)), dma((4, 4)),
            dma((4, 4)), dma((4, 4)),
        ],
        compiler_params=pltpu.CompilerParams(
            collective_id=0, has_side_effects=True, vmem_limit_bytes=40 * 1024 * 1024
        ),
        name="step",
    )(*args)


def per_device(
    pooled_grad,
    grad_scale,
    hot_slot,
    send_index,
    recv_row,
    cold_weight,
    cold_accum,
    hot_weight,
    hot_accum,
):
    return step(
        pooled_grad,
        send_index[0].T,
        grad_scale.T,
        hot_slot.transpose(1, 2, 0),
        recv_row[0].T,
        cold_weight,
        cold_accum,
        hot_weight,
        hot_accum,
    )


def solution(mesh):
    in_specs = (
        P(NODE_CHIP, None, None),
        P(NODE_CHIP, None),
        P(NODE_CHIP, None, None),
        P(NODE_CHIP, None, None),
        P(NODE_CHIP, None, None),
        P(None, NODE_CHIP, None),
        P(None, NODE_CHIP),
        P(),
        P(),
    )
    out_specs = (P(None, NODE_CHIP, None), P(None, NODE_CHIP), P(), P())
    return jax.shard_map(
        per_device, mesh=mesh, in_specs=in_specs, out_specs=out_specs, check_vma=False
    )
```

time: 148 us -> 66.9 us (0.45)
  Pallas kernels: 0 us -> 61.4 us
  waiting for transfers between devices: 45.4 us -> 0 us
  blocking collectives: 43.8 us -> 0 us
  other arithmetic: 18.9 us -> 0 us
  matrix products: 17.8 us -> 0 us
  starting transfers between devices: 9.7 us -> 0 us
  local copies, waits for them, and re-layouts: 10.6 us -> 4.54 us
    pallas_call x0 -> x1, Pallas kernels: none -> 61.4 us  [step(): pl.pallas_call(step_kernel, out_shape=tuple((jax.ShapeDtypeStruct(a.shape...]
    all_to_all x2 -> x0, waiting for transfers between devices: 45.4 us -> none  [the longest x1 37.4 us: in_one_piece(): lax.all_to_all(both, axis, split_axis=split_dim, concat_axis=concat_dim,...]
    all_to_all x3 -> x0, blocking collectives: 43.8 us -> none  [the longest x1 28.7 us: summed_rows(): lax.all_to_all(nearer, far, split_axis=0, concat_axis=0, tiled=True)]
    dot_general x5 -> x0, matrix products: 17.8 us -> none  [the longest x2 13 us: block_grad(): return jnp.dot(weights, arrived_rows, preferred_element_type=jnp.float32)]
    all_to_all x2 -> x0, starting transfers between devices: 9.7 us -> none  [the longest x1 5 us: in_one_piece(): lax.all_to_all(both, axis, split_axis=split_dim, concat_axis=concat_dim,...]
    sub x2 -> x0, other arithmetic: 6.8 us -> none  [adagrad(): weight - LEARN_RATE * grad / jnp.sqrt(accum_new)[..., None]]
    reduce_sum x5 -> x0, other arithmetic: 6.31 us -> none  [the longest x2 5.06 us: adagrad(): accum_new = accum + jnp.mean(grad * grad, axis=-1)]
    unnamed x20 -> x4, local copies, waits for them, and re-layouts: 0.99 us -> 4.54 us
  transfers between devices with their start and end apart: 2 -> 0, of which waited for: 2 -> 0; matrix products, arithmetic and copies ran while one was open for 8% -> 0% of each run, Pallas kernels for 0% -> 0%
where the time goes in v2:
time: 66.9 us; the launch traced here: 66.6 us
  Pallas kernels  61.4 us (92%)
  local copies, waits for them, and re-layouts  4.54 us (7%)
    pallas_call x1, Pallas kernels, step(): pl.pallas_call(step_kernel, out_shape=tuple((jax.ShapeDtypeStruct(a.shape...  61.4 us
    unnamed x4, local copies, waits for them, and re-layouts  4.54 us

profile of v2, /device:TPU:1, one launch (start us, length us, event | category | flops | bytes accessed | tf_op | source)
XLA Modules:
  0.0 66.6 jit_solution(10299774353135737787)
XLA Ops:
  0.6 61.4 %step.1 = (f32[4,1024,256]{2,1,0:T(8,128)S(1)}, f32[4,1024]{1,0:T(4,128)S(1)}, f32[4,512,256]{2,1,0:T(8,128)S(1)}, f32[4,512]{1,0:T(4,128)S(1)}) custom-call(bf16[64,4,256]{2,1,0:T(4,128)(2,1)} %rows_in.1, s32[32,128]{1,0:T(8,128)} %bitcast.8, bf16[4,64]{1,0:T(4,128)(2,1)} %bitcast.11, s32[4,2,64]{2,1,0:T(2,128)} %bitcast.10, s32[32,128]{1,0:T(8,128)} %bitcast.9, ...), custom_call_target="tpu_custom_call" | custom-call | tf_op jit(solution)/shard_map/step/pallas_call | solution.py:350
  62.1 2.0 %copy.17 = f32[4,1024,256]{2,1,0:T(8,128)} copy(f32[4,1024,256]{2,1,0:T(8,128)S(1)} %get-tuple-element.8) | data formatting | bytes 8388608
  64.1 0.6 copy.18
  64.7 1.3 %copy.19 = f32[4,512,256]{2,1,0:T(8,128)} copy(f32[4,512,256]{2,1,0:T(8,128)S(1)} %get-tuple-element.10) | data formatting | bytes 4194304
  66.0 0.6 copy.20

commit v3 on v2

--- a/solution.py
+++ b/solution.py
@@ -13,10 +13,10 @@
 ROW_STEP = 512
 F32 = jnp.float32
 BF16 = jnp.bfloat16
-FORWARD = (0, 3)
 SECOND = (
     (1, 0), (3, 0), (1, 1), (3, 1), (2, 0), (1, 3), (3, 3), (2, 1), (1, 2), (3, 2), (2, 3), (2, 2),
 )
+HELD = 6
 
 
 def iota(shape, dim):
@@ -33,18 +33,36 @@
     return jnp.transpose(jnp.concatenate([values, jnp.zeros((96, 128), F32)], axis=0))
 
 
-def adagrad_rows(value, weight, old):
+def columns_of(accum, columns):
     eye = iota((128, 128), 0) == iota((128, 128), 1)
-    mean = jnp.sum(value * value, axis=1, keepdims=True) * (1.0 / value.shape[1])
-    new = jnp.sum(jnp.where(eye, old, 0.0), axis=1, keepdims=True) + mean
-    flat = jnp.sum(jnp.where(eye, new, 0.0), axis=0, keepdims=True)
-    return weight - value * (LEARN_RATE / jnp.sqrt(new)), flat
+    for t in range(columns.shape[0]):
+        for n in range(columns.shape[1] // 128):
+            at = slice(n * 128, n * 128 + 128)
+            spread = jnp.where(eye, accum[t : t + 1, at], 0.0)
+            column = jnp.sum(spread, axis=1, keepdims=True)
+            columns[t, at, :] = jnp.broadcast_to(column, (128, 128))
+
+
+def rows_of(columns, accum):
+    eye = iota((128, 128), 0) == iota((128, 128), 1)
+    for t in range(columns.shape[0]):
+        for n in range(columns.shape[1] // 128):
+            at = slice(n * 128, n * 128 + 128)
+            row = jnp.sum(jnp.where(eye, columns[t, at, :], 0.0), axis=0, keepdims=True)
+            accum[t : t + 1, at] = row
+
+
+def adagrad_rows(grad, weight, old):
+    mean = jnp.sum(grad * grad, axis=1, keepdims=True) * (1.0 / grad.shape[1])
+    new = old + mean
+    rate = LEARN_RATE / jnp.sqrt(new)
+    return weight - grad * jnp.concatenate([rate, rate], axis=1), new
 
 
 def step_kernel(
     rows_in, send_in, scale_in, hot_in, recv_in, cold_weight, cold_accum_in, hot_weight, hot_accum_in,
     cold_new, cold_accum_new, hot_new, hot_accum_new,
-    g, s, ssc, arrived, scr, hp, hr, hs, hz, hot_grad, st, tt, cold_w, hot_w,
+    g, s, ssc, arrived, scr, hp, hr, hs, hz, hot_grad, st, tt, cold_w, hot_w, cold_sum, hot_sum,
     rows, send_t, scale_t, hot_t, recv_t, cold_accum, hot_accum, l0, s1, r1, s2, r2, s3, r3, s4, r4, s5, r5, s6, r6, s7, r7, s8, r8, s9, r9,
 ):
     z = lax.axis_index("node")
@@ -156,7 +174,7 @@
     own = g.at[p2, p1]
     for d in (1, 3, 2):
         send(own, own, s1.at[d], r1.at[d], plane((p1 + d) % 4, p2))
-    for d in (1, 3):
+    for d in (1, 3, 2):
         send(own, own, s2.at[d, 0], r2.at[d, 0], plane(p1, (p2 + d) % 4))
     for copy in later:
         copy.start()
@@ -216,7 +234,7 @@
             wanted = wanted + (pltpu.roll(row, 32 * b, 1) if b else row)
         return wanted, scr[q, a], arrived[q, :, a].reshape(128, SEL)
 
-    def scatter(j, first=False, last=False):
+    def chunk(j):
         for m in range(1, 8):
             src, cc = from_z(m)
             a = (y + cc * (x - y) + 4 - j) % 4
@@ -229,6 +247,10 @@
         wanted = jnp.concatenate([p[0] for p in parts], axis=1)
         scales = jnp.concatenate([p[1] for p in parts], axis=1)
         values = jnp.concatenate([p[2] for p in parts], axis=0)
+        return wanted, scales, values
+
+    def scatter(parts, low_step, high_step, first=False, last=False):
+        wanted, scales, values = parts
         level = iota((ROW_STEP, 1024), 0).astype(F32)
 
         def step(i, carry):
@@ -241,102 +263,90 @@
             if not last:
                 cold_new[t, pl.ds(low, ROW_STEP), :] = total
                 return carry
-            for n in range(ROW_STEP // 128):
-                at = pl.ds(pl.multiple_of(low + n * 128, 128), 128)
-                kept = cold_accum_new[:, at]
-                fresh, flat = adagrad_rows(
-                    total[n * 128 : n * 128 + 128], cold_w[t, at, :], row_of(cold_accum[:, at], t)
-                )
-                cold_new[t, at, :] = fresh
-                cold_accum_new[:, at] = jnp.where(iota((4, 128), 0) == t, flat, kept)
+            at = pl.ds(low, ROW_STEP)
+            fresh, new = adagrad_rows(total, cold_w[t, at, :], cold_sum[t, at, :])
+            cold_new[t, at, :] = fresh
+            cold_sum[t, at, :] = new
             return carry
 
-        lax.fori_loop(0, 4096 // ROW_STEP, step, 0)
+        lax.fori_loop(low_step, high_step, step, 0)
 
     select(p2, p1, (0, 0))
     add_hot(p2, p1)
+    for copy in later:
+        copy.wait()
+    tt[...] = turned(recv_t[...])
+    columns_of(cold_accum, cold_sum)
+    columns_of(hot_accum, hot_sum)
     for j in (1, 3, 2):
         a = (p1 + 4 - j) % 4
         landed(g.at[p2, a], s1.at[j], r1.at[j])
-        for d in (1, 3):
+        for d in (1, 3, 2):
             send(g.at[p2, a], g.at[p2, a], s2.at[d, j], r2.at[d, j], plane(p1, (p2 + d) % 4))
         select(p2, a, (0, j))
         add_hot(p2, a)
 
-    for d, j in SECOND:
+    def pass_on(d, j):
+        select((p2 + 4 - d) % 4, (p1 + 4 - j) % 4, (d, j))
+        if d == 2:
+            send_scales(j)
+
+    for n, (d, j) in enumerate(SECOND):
         b, a = (p2 + 4 - d) % 4, (p1 + 4 - j) % 4
         landed(g.at[b, a], s2.at[d, j], r2.at[d, j])
-        onward = 1 if j in FORWARD else 3
-        if d == onward:
-            send(g.at[b, a], g.at[b, a], s2.at[2, j], r2.at[2, j], plane(p1, (p2 + d) % 4))
         add_hot(b, a)
-        if (d, j) == SECOND[-1]:
-            send(hp.at[twin_part], hr, s5.at[0], r5.at[0], twin)
-        select(b, a, (d, j))
-        if d == 2:
-            send_scales(j)
-
-    for copy in later:
-        copy.wait()
-    tt[...] = turned(recv_t[...])
-    scatter(0, first=True)
-
+        if n < len(SECOND) - HELD:
+            pass_on(d, j)
+    send(hp.at[twin_part], hr, s5.at[0], r5.at[0], twin)
+    for d, j in SECOND[-HELD : 2 - HELD]:
+        pass_on(d, j)
     landed(hr, s5.at[0], r5.at[0])
     hs[...] = hp[part] + hr[...]
     for m in (2, 6, 4):
         send(hs, hz.at[m // 2], s6.at[m // 2], r6.at[m // 2], along_z(m)[1])
-
-    scatter(1)
-
+    for d, j in SECOND[2 - HELD :]:
+        pass_on(d, j)
+
+    steps = 4096 // ROW_STEP
+    scatter(chunk(0), 0, steps, first=True)
     for m in (1, 3, 2):
         landed(hz.at[m], s6.at[m], r6.at[m])
     hot_grad[x, y, part] = hs[...] + hz[1] + hz[2] + hz[3]
     piece = hot_grad.at[x, y, part]
     for d in (1, 3, 2):
         send(piece, piece, s7.at[d], r7.at[d], plane((p1 + d) % 4, p2))
-    for d in (1, 3):
+    for d in (1, 3, 2):
         send(piece, piece, s8.at[d, 0], r8.at[d, 0], plane(p1, (p2 + d) % 4))
     send(piece, piece, s9.at[0, 0], r9.at[0, 0], twin)
-
-    scatter(3)
-
+    scatter(chunk(1), 0, steps)
     for j in (1, 3, 2):
         xx, yy = share((p1 + 4 - j) % 4, p2)
         piece = hot_grad.at[xx, yy, part]
         landed(piece, s7.at[j], r7.at[j])
-        for d in (1, 3):
+        for d in (1, 3, 2):
             send(piece, piece, s8.at[d, j], r8.at[d, j], plane(p1, (p2 + d) % 4))
         send(piece, piece, s9.at[0, j], r9.at[0, j], twin)
-
-    def second_piece(d, j):
-        xx, yy = share((p1 + 4 - j) % 4, (p2 + 4 - d) % 4)
-        piece = hot_grad.at[xx, yy, part]
-        landed(piece, s8.at[d, j], r8.at[d, j])
-        onward = 1 if j in FORWARD else 3
-        if d == onward:
-            send(piece, piece, s8.at[2, j], r8.at[2, j], plane(p1, (p2 + d) % 4))
-        send(piece, piece, s9.at[d, j], r9.at[d, j], twin)
-
-    second_piece(1, 0)
-    second_piece(3, 0)
-    scatter(2, last=True)
-    for d, j in SECOND[2:]:
-        second_piece(d, j)
-    for d in range(4):
-        for j in range(4):
+    scatter(chunk(3), 0, steps)
+    scatter(chunk(2), 0, steps, last=True)
+    rows_of(cold_sum, cold_accum_new)
+    for j in (0, 1, 3, 2):
+        for d in (1, 3, 2):
+            xx, yy = share((p1 + 4 - j) % 4, (p2 + 4 - d) % 4)
+            piece = hot_grad.at[xx, yy, part]
+            landed(piece, s8.at[d, j], r8.at[d, j])
+            send(piece, piece, s9.at[d, j], r9.at[d, j], twin)
+    for j in (0, 1, 3, 2):
+        for d in (0, 1, 3, 2):
             q1 = (x + c * (y - x) + 4 - j) % 4
             q2 = (y + c * (x - y) + 4 - d) % 4
             xx = q1 + c * (q2 - q1)
             yy = q2 + c * (q1 - q2)
             landed(hot_grad.at[xx, yy, twin_part], s9.at[d, j], r9.at[d, j])
     for t in range(4):
-        for n in range(4):
-            at = slice(n * 128, n * 128 + 128)
-            fresh, flat = adagrad_rows(
-                hot_grad[t, n].reshape(128, SEL), hot_w[t, at, :], hot_accum[t : t + 1, at]
-            )
-            hot_new[t, at, :] = fresh
-            hot_accum_new[t : t + 1, at] = flat
+        fresh, new = adagrad_rows(hot_grad[t].reshape(512, SEL), hot_w[t], hot_sum[t])
+        hot_new[t] = fresh
+        hot_sum[t] = new
+    rows_of(hot_sum, hot_accum_new)
     for copy in sends:
         copy.wait_send()
 
@@ -367,6 +377,8 @@
             pltpu.VMEM((128, 128), F32),
             pltpu.VMEM(outs[0].shape, F32),
             pltpu.VMEM(outs[2].shape, F32),
+            pltpu.VMEM((*outs[0].shape[:2], 128), F32),
+            pltpu.VMEM((*outs[2].shape[:2], 128), F32),
             *(pltpu.VMEM(a.shape, a.dtype) for a in (*args[:5], args[6], args[8])),
             dma((9,)),
             dma((4,)), dma((4,)),
@@ -386,6 +398,29 @@
     )(*args)
 
 
+def leave_kernel(*refs):
+    sem = refs[-1]
+    copies = [
+        pltpu.make_async_copy(refs[n], refs[4 + n], sem.at[n]) for n in range(4)
+    ]
+    for copy in copies:
+        copy.start()
+    for copy in copies:
+        copy.wait()
+
+
+def leave(*arrays):
+    return pl.pallas_call(
+        leave_kernel,
+        out_shape=tuple(jax.ShapeDtypeStruct(a.shape, a.dtype) for a in arrays),
+        in_specs=[pl.BlockSpec(memory_space=pltpu.VMEM)] * 4,
+        out_specs=(pl.BlockSpec(memory_space=pl.ANY),) * 4,
+        scratch_shapes=[pltpu.SemaphoreType.DMA((4,))],
+        compiler_params=pltpu.CompilerParams(vmem_limit_bytes=16 * 1024 * 1024),
+        name="leave",
+    )(*arrays)
+
+
 def per_device(
     pooled_grad,
     grad_scale,
@@ -397,7 +432,7 @@
     hot_weight,
     hot_accum,
 ):
-    return step(
+    results = step(
         pooled_grad,
         send_index[0].T,
         grad_scale.T,
@@ -408,6 +443,7 @@
         hot_weight,
         hot_accum,
     )
+    return leave(*results)
 
 
 def solution(mesh):

time: 66.9 us -> 60.5 us (0.904)
  local copies, waits for them, and re-layouts: 4.54 us -> 0 us
  Pallas kernels: 61.4 us -> 59.7 us
    unnamed x4 -> x0, local copies, waits for them, and re-layouts: 4.54 us -> none
    pallas_call x1, Pallas kernels: 61.4 us -> 56.9 us  [step(): pl.pallas_call(step_kernel, out_shape=tuple((jax.ShapeDtypeStruct(a.shape...]
    pallas_call x0 -> x1, Pallas kernels: none -> 2.74 us  [leave(): pl.pallas_call(leave_kernel, out_shape=tuple((jax.ShapeDtypeStruct(a.shap...]
where the time goes in v3:
time: 60.5 us; the launch traced here: 60.3 us
  Pallas kernels  59.7 us (99%)
  between operations  0.64 us (1%)
    pallas_call x1, Pallas kernels, step(): pl.pallas_call(step_kernel, out_shape=tuple((jax.ShapeDtypeStruct(a.shape...  56.9 us
    pallas_call x1, Pallas kernels, leave(): pl.pallas_call(leave_kernel, out_shape=tuple((jax.ShapeDtypeStruct(a.shap...  2.74 us

profile of v3, /device:TPU:1, one launch (start us, length us, event | category | flops | bytes accessed | tf_op | source)
XLA Modules:
  0.0 60.3 jit_solution(15507187454169886836)
XLA Ops:
  0.6 56.9 %step.1 = (f32[4,1024,256]{2,1,0:T(8,128)S(1)}, f32[4,1024]{1,0:T(4,128)S(1)}, f32[4,512,256]{2,1,0:T(8,128)S(1)}, f32[4,512]{1,0:T(4,128)S(1)}) custom-call(bf16[64,4,256]{2,1,0:T(4,128)(2,1)} %rows_in.1, s32[32,128]{1,0:T(8,128)} %bitcast.8, bf16[4,64]{1,0:T(4,128)(2,1)} %bitcast.11, s32[4,2,64]{2,1,0:T(2,128)} %bitcast.10, s32[32,128]{1,0:T(8,128)} %bitcast.9, ...), custom_call_target="tpu_custom_call" | custom-call | tf_op jit(solution)/shard_map/step/pallas_call | solution.py:360
  57.6 2.7 %leave.1 = (f32[4,1024,256]{2,1,0:T(8,128)}, f32[4,1024]{1,0:T(4,128)}, f32[4,512,256]{2,1,0:T(8,128)}, f32[4,512]{1,0:T(4,128)}) custom-call(f32[4,1024,256]{2,1,0:T(8,128)S(1)} %get-tuple-element.8.refs_0_, f32[4,1024]{1,0:T(4,128)S(1)} %get-tuple-element.9.refs_1_, f32[4,512,256]{2,1,0:T(8,128)S(1)} %get-tuple-element.10.refs_2_, ...), custom_call_target="tpu_custom_call" | custom-call | tf_op jit(solution)/shard_map/leave/pallas_call | solution.py:413

commit v4 on v3

--- a/solution.py
+++ b/solution.py
@@ -13,10 +13,6 @@
 ROW_STEP = 512
 F32 = jnp.float32
 BF16 = jnp.bfloat16
-SECOND = (
-    (1, 0), (3, 0), (1, 1), (3, 1), (2, 0), (1, 3), (3, 3), (2, 1), (1, 2), (3, 2), (2, 3), (2, 2),
-)
-HELD = 6
 
 
 def iota(shape, dim):
@@ -63,7 +59,7 @@
     rows_in, send_in, scale_in, hot_in, recv_in, cold_weight, cold_accum_in, hot_weight, hot_accum_in,
     cold_new, cold_accum_new, hot_new, hot_accum_new,
     g, s, ssc, arrived, scr, hp, hr, hs, hz, hot_grad, st, tt, cold_w, hot_w, cold_sum, hot_sum,
-    rows, send_t, scale_t, hot_t, recv_t, cold_accum, hot_accum, l0, s1, r1, s2, r2, s3, r3, s4, r4, s5, r5, s6, r6, s7, r7, s8, r8, s9, r9,
+    rows, send_t, scale_t, hot_t, recv_t, cold_accum, hot_accum, l0, s1, r1, s2, r2, s3, r3, s4, r4, s5, r5, s6, r6, s7, r7, s8, r8, s9, r9, sa, ra,
 ):
     z = lax.axis_index("node")
     k = lax.axis_index("chip")
@@ -121,8 +117,11 @@
 
     for copy in first:
         copy.wait()
-    g[p2, p1, 0:SEL, :] = rows[...].astype(F32).reshape(SEL, SEL).astype(BF16)
-    st[...] = turned(send_t[...])
+    by_sample = rows[...].astype(F32)
+    for t in range(4):
+        g[p2, p1, t * 64 : t * 64 + 64, :] = by_sample[:, t, :].astype(BF16)
+    picks = send_t[...]
+    st[...] = turned((picks % 4) * 64 + picks // 4)
     halves = []
     for half in range(2):
         total = jnp.zeros((16, 128), F32)
@@ -148,10 +147,7 @@
                 axis=0,
             )
         )
-    info = jnp.concatenate(pieces, axis=1).astype(BF16)
-    from_lane = iota((SEL, SEL), 0)
-    order = jnp.where((from_lane % 64) * 4 + from_lane // 64 == iota((SEL, SEL), 1), 1.0, 0.0)
-    info = jnp.dot(info, order.astype(BF16), preferred_element_type=F32)
+    info = jnp.concatenate(pieces, axis=1)
     g[p2, p1, SEL + 16 : SEL + 32, :] = jnp.concatenate(
         [info, jnp.zeros((8, SEL), F32)], axis=0
     ).astype(BF16)
@@ -182,7 +178,8 @@
     lanes = iota((SEL, SEL), 1).astype(F32)
     same_owner = iota((8, SEL), 0) == iota((8, SEL), 1) // 32
     quarter = iota((8, 128), 1) // 32
-    levels = iota((128, SEL), 0).astype(F32)
+    levels = iota((128, 64), 0).astype(F32)
+    table = pl.ds(pl.multiple_of(x * 64, 64), 64)
     totals = [jnp.zeros((8, 128), F32)] * 4
     hp[...] = jnp.zeros_like(hp)
 
@@ -217,12 +214,13 @@
         scr[mine, a] = ssc[a, mine]
 
     def add_hot(b, a):
-        info = g[b, a, SEL + 16 : SEL + 32, :].astype(F32)
+        info = pltpu.roll(g[b, a, SEL + 16 : SEL + 32, :].astype(F32), (SEL - x * 64) % SEL, 1)
+        info = info[:, 0:64]
         at0 = jnp.where(info[0:1] == column.astype(F32), info[1:2], -1.0)
         at1 = jnp.where(info[2:3] == column.astype(F32), info[3:4], -1.0)
         scale = info[4:5]
         weight = jnp.where(levels == at0, scale, 0.0) + jnp.where(levels == at1, scale, 0.0)
-        total = jnp.dot(weight.astype(BF16), g[b, a, 0:SEL, :], preferred_element_type=F32)
+        total = jnp.dot(weight.astype(BF16), g[b, a, table, :], preferred_element_type=F32)
         hp[...] += total.reshape(8, 16, SEL)
 
     def gathered(q, j):
@@ -271,6 +269,24 @@
 
         lax.fori_loop(low_step, high_step, step, 0)
 
+    def piece_of(b, a, n, xx):
+        if n == 4:
+            return g.at[b, a, pl.ds(SEL, 32)]
+        return g.at[b, a, pl.ds(pl.multiple_of(((xx + n) % 4) * 64, 64), 64)]
+
+    def forward(d, j, parts):
+        a = (p1 + 4 - j) % 4
+        far = share(p1, (p2 + d) % 4)[0]
+        for n in parts:
+            ref = piece_of(p2, a, n, far)
+            send(ref, ref, sa.at[d, j, n], ra.at[d, j, n], plane(p1, (p2 + d) % 4))
+
+    def arrives(d, j, parts):
+        for n in parts:
+            landed(
+                piece_of((p2 + 4 - d) % 4, (p1 + 4 - j) % 4, n, x), sa.at[d, j, n], ra.at[d, j, n]
+            )
+
     select(p2, p1, (0, 0))
     add_hot(p2, p1)
     for copy in later:
@@ -282,7 +298,7 @@
         a = (p1 + 4 - j) % 4
         landed(g.at[p2, a], s1.at[j], r1.at[j])
         for d in (1, 3, 2):
-            send(g.at[p2, a], g.at[p2, a], s2.at[d, j], r2.at[d, j], plane(p1, (p2 + d) % 4))
+            forward(d, j, (0, 4))
         select(p2, a, (0, j))
         add_hot(p2, a)
 
@@ -291,24 +307,28 @@
         if d == 2:
             send_scales(j)
 
-    for n, (d, j) in enumerate(SECOND):
-        b, a = (p2 + 4 - d) % 4, (p1 + 4 - j) % 4
-        landed(g.at[b, a], s2.at[d, j], r2.at[d, j])
-        add_hot(b, a)
-        if n < len(SECOND) - HELD:
-            pass_on(d, j)
+    for j in (1, 3, 2):
+        for d in (1, 3, 2):
+            forward(d, j, (1, 2, 3))
+    for d in (1, 3, 2):
+        b = (p2 + 4 - d) % 4
+        landed(g.at[b, p1], s2.at[d, 0], r2.at[d, 0])
+        add_hot(b, p1)
+        pass_on(d, 0)
+    for j in (1, 3, 2):
+        for d in (1, 3, 2):
+            arrives(d, j, (0, 4))
+            add_hot((p2 + 4 - d) % 4, (p1 + 4 - j) % 4)
     send(hp.at[twin_part], hr, s5.at[0], r5.at[0], twin)
-    for d, j in SECOND[-HELD : 2 - HELD]:
-        pass_on(d, j)
     landed(hr, s5.at[0], r5.at[0])
     hs[...] = hp[part] + hr[...]
     for m in (2, 6, 4):
         send(hs, hz.at[m // 2], s6.at[m // 2], r6.at[m // 2], along_z(m)[1])
-    for d, j in SECOND[2 - HELD :]:
-        pass_on(d, j)
-
-    steps = 4096 // ROW_STEP
-    scatter(chunk(0), 0, steps, first=True)
+    for j in (1, 3, 2):
+        for d in (1, 3, 2):
+            arrives(d, j, (1, 2, 3))
+            pass_on(d, j)
+
     for m in (1, 3, 2):
         landed(hz.at[m], s6.at[m], r6.at[m])
     hot_grad[x, y, part] = hs[...] + hz[1] + hz[2] + hz[3]
@@ -318,7 +338,8 @@
     for d in (1, 3, 2):
         send(piece, piece, s8.at[d, 0], r8.at[d, 0], plane(p1, (p2 + d) % 4))
     send(piece, piece, s9.at[0, 0], r9.at[0, 0], twin)
-    scatter(chunk(1), 0, steps)
+    steps = 4096 // ROW_STEP
+    scatter(chunk(0), 0, steps, first=True)
     for j in (1, 3, 2):
         xx, yy = share((p1 + 4 - j) % 4, p2)
         piece = hot_grad.at[xx, yy, part]
@@ -326,15 +347,16 @@
         for d in (1, 3, 2):
             send(piece, piece, s8.at[d, j], r8.at[d, j], plane(p1, (p2 + d) % 4))
         send(piece, piece, s9.at[0, j], r9.at[0, j], twin)
+    scatter(chunk(1), 0, steps)
     scatter(chunk(3), 0, steps)
-    scatter(chunk(2), 0, steps, last=True)
-    rows_of(cold_sum, cold_accum_new)
     for j in (0, 1, 3, 2):
         for d in (1, 3, 2):
             xx, yy = share((p1 + 4 - j) % 4, (p2 + 4 - d) % 4)
             piece = hot_grad.at[xx, yy, part]
             landed(piece, s8.at[d, j], r8.at[d, j])
             send(piece, piece, s9.at[d, j], r9.at[d, j], twin)
+    scatter(chunk(2), 0, steps, last=True)
+    rows_of(cold_sum, cold_accum_new)
     for j in (0, 1, 3, 2):
         for d in (0, 1, 3, 2):
             q1 = (x + c * (y - x) + 4 - j) % 4
@@ -390,6 +412,7 @@
             dma((4,)), dma((4,)),
             dma((4, 4)), dma((4, 4)),
             dma((4, 4)), dma((4, 4)),
+            dma((4, 4, 5)), dma((4, 4, 5)),
         ],
         compiler_params=pltpu.CompilerParams(
             collective_id=0, has_side_effects=True, vmem_limit_bytes=40 * 1024 * 1024

time: 60.5 us -> 56.8 us (0.939)
  Pallas kernels: 59.7 us -> 56 us
    pallas_call x1, Pallas kernels: 56.9 us -> 53.2 us  [step(): pl.pallas_call(step_kernel, out_shape=tuple((jax.ShapeDtypeStruct(a.shape...]
where the time goes in v4:
time: 56.8 us; the launch traced here: 56.6 us
  Pallas kernels  56 us (99%)
  between operations  0.64 us (1%)
    pallas_call x1, Pallas kernels, step(): pl.pallas_call(step_kernel, out_shape=tuple((jax.ShapeDtypeStruct(a.shape...  53.2 us
    pallas_call x1, Pallas kernels, leave(): pl.pallas_call(leave_kernel, out_shape=tuple((jax.ShapeDtypeStruct(a.shap...  2.74 us

profile of v4, /device:TPU:1, one launch (start us, length us, event | category | flops | bytes accessed | tf_op | source)
XLA Modules:
  0.0 56.6 jit_solution(5217918237137111733)
XLA Ops:
  0.6 53.2 %step.1 = (f32[4,1024,256]{2,1,0:T(8,128)S(1)}, f32[4,1024]{1,0:T(4,128)S(1)}, f32[4,512,256]{2,1,0:T(8,128)S(1)}, f32[4,512]{1,0:T(4,128)S(1)}) custom-call(bf16[64,4,256]{2,1,0:T(4,128)(2,1)} %rows_in.1, s32[32,128]{1,0:T(8,128)} %bitcast.8, bf16[4,64]{1,0:T(4,128)(2,1)} %bitcast.11, s32[4,2,64]{2,1,0:T(2,128)} %bitcast.10, s32[32,128]{1,0:T(8,128)} %bitcast.9, ...), custom_call_target="tpu_custom_call" | custom-call | tf_op jit(solution)/shard_map/step/pallas_call | solution.py:382
  53.9 2.7 %leave.1 = (f32[4,1024,256]{2,1,0:T(8,128)}, f32[4,1024]{1,0:T(4,128)}, f32[4,512,256]{2,1,0:T(8,128)}, f32[4,512]{1,0:T(4,128)}) custom-call(f32[4,1024,256]{2,1,0:T(8,128)S(1)} %get-tuple-element.8.refs_0_, f32[4,1024]{1,0:T(4,128)S(1)} %get-tuple-element.9.refs_1_, f32[4,512,256]{2,1,0:T(8,128)S(1)} %get-tuple-element.10.refs_2_, ...), custom_call_target="tpu_custom_call" | custom-call | tf_op jit(solution)/shard_map/leave/pallas_call | solution.py:436

commit v5 on v4

--- a/solution.py
+++ b/solution.py
@@ -10,7 +10,8 @@
 LEARN_RATE = 0.5
 SEL = 256
 BLOCK_ROWS = 288
-ROW_STEP = 512
+ROW_STEP = 1024
+PER_TABLE = 1024 // ROW_STEP
 F32 = jnp.float32
 BF16 = jnp.bfloat16
 
@@ -252,7 +253,7 @@
         level = iota((ROW_STEP, 1024), 0).astype(F32)
 
         def step(i, carry):
-            t, low = i // 2, pl.multiple_of((i % 2) * ROW_STEP, ROW_STEP)
+            t, low = i // PER_TABLE, pl.multiple_of((i % PER_TABLE) * ROW_STEP, ROW_STEP)
             base = (i * ROW_STEP).astype(F32)
             weight = jnp.where(level == wanted - base, scales, 0.0).astype(BF16)
             total = jnp.dot(weight, values, preferred_element_type=F32)

time: 56.8 us -> 55.1 us (0.970)
  Pallas kernels: 56 us -> 54.3 us
    pallas_call x1, Pallas kernels: 53.2 us -> 51.5 us  [step(): pl.pallas_call(step_kernel, out_shape=tuple((jax.ShapeDtypeStruct(a.shape...]
where the time goes in v5:
time: 55.1 us; the launch traced here: 54.9 us
  Pallas kernels  54.3 us (99%)
  between operations  0.64 us (1%)
    pallas_call x1, Pallas kernels, step(): pl.pallas_call(step_kernel, out_shape=tuple((jax.ShapeDtypeStruct(a.shape...  51.5 us
    pallas_call x1, Pallas kernels, leave(): pl.pallas_call(leave_kernel, out_shape=tuple((jax.ShapeDtypeStruct(a.shap...  2.74 us

profile of v5, /device:TPU:1, one launch (start us, length us, event | category | flops | bytes accessed | tf_op | source)
XLA Modules:
  0.0 54.9 jit_solution(11375023925417839625)
XLA Ops:
  0.6 51.5 %step.1 = (f32[4,1024,256]{2,1,0:T(8,128)S(1)}, f32[4,1024]{1,0:T(4,128)S(1)}, f32[4,512,256]{2,1,0:T(8,128)S(1)}, f32[4,512]{1,0:T(4,128)S(1)}) custom-call(bf16[64,4,256]{2,1,0:T(4,128)(2,1)} %rows_in.1, s32[32,128]{1,0:T(8,128)} %bitcast.8, bf16[4,64]{1,0:T(4,128)(2,1)} %bitcast.11, s32[4,2,64]{2,1,0:T(2,128)} %bitcast.10, s32[32,128]{1,0:T(8,128)} %bitcast.9, ...), custom_call_target="tpu_custom_call" | custom-call | tf_op jit(solution)/shard_map/step/pallas_call | solution.py:383
  52.2 2.7 %leave.1 = (f32[4,1024,256]{2,1,0:T(8,128)}, f32[4,1024]{1,0:T(4,128)}, f32[4,512,256]{2,1,0:T(8,128)}, f32[4,512]{1,0:T(4,128)}) custom-call(f32[4,1024,256]{2,1,0:T(8,128)S(1)} %get-tuple-element.8.refs_0_, f32[4,1024]{1,0:T(4,128)S(1)} %get-tuple-element.9.refs_1_, f32[4,512,256]{2,1,0:T(8,128)S(1)} %get-tuple-element.10.refs_2_, ...), custom_call_target="tpu_custom_call" | custom-call | tf_op jit(solution)/shard_map/leave/pallas_call | solution.py:437
